TPU v7x, 256 devices: a whole 4x4x8 slice. The times are simulated.
256 devices in a mesh: dom: 32 (over y, z), sub: 8 (over x, core).
Axes of the slice: x: 4, y: 4, z: 8, core: 2. Of those that a mesh axis runs over, the one named last changes fastest.
Arguments:
- positions: float32 [16384, 3, 256], P(('dom', 'sub')), may hold values from -6 to 6
- time_bins: int32 [16384, 256], P(('dom', 'sub')), may hold values from 0 to 5
- home_groups: int32 [16384], P(('dom', 'sub')), may hold values from 0 to 63
- targets: int32 [16384, 4], P(('dom', 'sub')), may hold values from -1 to 31, as said below
- target_groups: int32 [16384, 4], P(('dom', 'sub')), may hold values from 0 to 63
- node_pos: float32 [3, 1048576], P(None, ('dom', 'sub')), may hold values from -6 to 6
- node_mass: float32 [1048576], P(('dom', 'sub')), may hold values from 0.2 to 2
- node_lists: int32 [2048, 256], P('dom'), may hold values from 0 to 32767
- list_counts: int32 [2048], P('dom'), may hold values from 64 to 256, as said below
Outputs:
- forces: float32 [16384, 3, 256], P(('dom', 'sub'))
Inputs may be any that keep to these rules, and one draw needn't show every extreme that they name: `targets`: row b names the remote domains that block b visits, each at most once and never its own domain b // 512; -1 marks an unused entry, in any column. The rows of one device name one domain at most 8 times, and some device names some domain exactly 8 times in every draw. The rows of one domain's 8 devices together name one domain at most 16 times, and this is reached in every draw. `list_counts`: each domain has at least one list with all 256 entries valid.
All inputs are finite; a program needn't handle non-finite values.
Results may differ from a plain program's by a relative error of at most 0.0003.
Values sent between devices are 32-bit elements; how exact they have to be, the bound alone decides.
No kernel may reach another device: no remote copies, remote signals or barrier semaphores. Data moves between devices by JAX's collectives and lax.ppermute only.
A program may use at most 128 MiB of HBM per device.

v0:
```python
import math

import jax
import jax.numpy as jnp
from jax import lax
from jax.experimental import pallas as pl
from jax.experimental.pallas import tpu as pltpu
from jax.sharding import PartitionSpec as P


CUR_BIN = 2
SOFT = 0.04
F32 = jnp.float32
BF16 = jnp.bfloat16
I32 = jnp.int32

BETA = 0.3
POLY = (
    0.000177460321,
    0.334470999,
    0.374323182,
    0.116028516,
    0.555240376,
    -0.510157925,
    0.129925288,
)
LEAD = POLY[6]
MONIC = tuple(c / LEAD for c in POLY[:6])
TAIL = 1.0 / (BETA * math.sqrt(math.pi) * LEAD)
DECAY = -math.log2(math.e) / (4.0 * BETA * BETA)
OUT_SCALE = BETA * BETA * LEAD

WIDTHS = (128, 144, 160, 192, 256)
KI = 6
VMEM = pltpu.VMEM
SMEM = pltpu.SMEM
SLOTS = 8


def vspec():
    return pl.BlockSpec(memory_space=VMEM)


def sspec():
    return pl.BlockSpec(memory_space=SMEM)


def hspec():
    return pl.BlockSpec(memory_space=pltpu.MemorySpace.HBM)


def nt_dot(a, b):
    return lax.dot_general(a, b, (((1,), (1,)), ((), ())), preferred_element_type=F32)


def split3(v):
    first = v.astype(BF16).astype(F32)
    rest = v - first
    second = rest.astype(BF16).astype(F32)
    return first, second, rest - second


def fetch(sources, buffers, sems):
    copies = [pltpu.make_async_copy(a, b, sems.at[k]) for k, (a, b) in enumerate(zip(sources, buffers))]
    for copy in copies:
        copy.start()
    return copies


def request_kernel(*refs):
    sources, (req_ref, slot_ref, nodes_ref), held, sems = refs[:5], refs[5:8], refs[8:13], refs[13]
    for copy in fetch(sources, held, sems):
        copy.wait()
    targets_ref, groups_ref, counts_ref, pos_ref, mass_ref = held
    most = targets_ref.shape[0]
    pairs = most * targets_ref.shape[1]
    domains = req_ref.shape[0]

    def in_line(ref):
        return jnp.concatenate([ref[v : v + 1, :] for v in range(most)], axis=1).astype(F32)

    dest = in_line(targets_ref)
    along = jnp.broadcast_to(dest, (pairs, pairs))
    down = jnp.transpose(along)
    earlier = lax.broadcasted_iota(I32, (pairs, pairs), 0) < lax.broadcasted_iota(I32, (pairs, pairs), 1)
    rank = jnp.sum(jnp.where((along == down) & earlier, 1.0, 0.0), axis=0, keepdims=True)
    slot = jnp.where(dest >= 0, dest * SLOTS + rank, -1.0)
    slot_ref[...] = slot.astype(I32)
    dom_id = lax.broadcasted_iota(I32, (domains, pairs), 0).astype(F32)
    asked = in_line(groups_ref) + 1.0
    by_dom = jnp.where(dom_id == dest, asked, 0.0).astype(BF16)
    lane_id = lax.broadcasted_iota(I32, (128, pairs), 0).astype(F32)
    by_rank = jnp.where(lane_id == rank, 1.0, 0.0).astype(BF16)
    wanted = nt_dot(by_dom, by_rank).astype(I32)
    half = counts_ref.shape[1]
    tail = jnp.concatenate([jnp.zeros((1, 128 - half), I32), counts_ref[...]], axis=1)
    lanes = lax.broadcasted_iota(I32, (domains, 128), 1)
    req_ref[...] = jnp.where(lanes < 128 - half, wanted, jnp.broadcast_to(tail, (domains, 128)))
    for r in range(nodes_ref.shape[1]):
        for c in range(3):
            nodes_ref[c, r : r + 1, :] = pos_ref[c : c + 1, 128 * r : 128 * r + 128]
        nodes_ref[3, r : r + 1, :] = mass_ref[0:1, 128 * r : 128 * r + 128]


def list_kernel(*refs):
    chips = len(refs) - 10
    node_refs = refs[:chips]
    lists_hbm, counts_hbm, tab_ref, table_ref, lists_ref, counts_ref, one_ref, *found_refs, sems = refs[chips:]
    _, rows, _ = node_refs[0].shape
    total = chips * rows
    octets = lists_ref.shape[0] // 8
    copies = fetch((lists_hbm, counts_hbm), (lists_ref, counts_ref), sems)
    sharers = lax.axis_size("sub")
    bases = [lax.rem(lax.axis_index("sub") + sharers - 2 * j, sharers) * rows for j in range(chips)]
    for c in range(3):
        tall = jnp.concatenate([ref[c] for ref in node_refs], axis=0)
        parts = split3(jnp.transpose(tall) * BETA)
        for k in range(3):
            table_ref[128 * c : 128 * c + 128, total * k : total * k + total] = parts[k].astype(BF16)
    for copy in copies:
        copy.wait()
    row16 = lax.broadcasted_iota(I32, (16, 256), 0)
    row8 = lax.broadcasted_iota(I32, (8, 256), 0)
    entry_id = lax.broadcasted_iota(I32, (1, 256), 1)

    def gather(i, carry):
        first = pl.multiple_of(i * 8, 8)
        lane = [lists_ref[pl.ds(first, 8), 128 * h : 128 * h + 128] & 127 for h in range(2)]
        row = [lists_ref[pl.ds(first, 8), 128 * h : 128 * h + 128] >> 7 for h in range(2)]

        def search(k):
            at = jnp.broadcast_to(lists_ref[pl.ds(first + k, 1), :] >> 7, (16, 256))
            for j in range(chips):
                for q in range(0, rows, 16):
                    piece = jnp.where(row16 == at - (bases[j] + q), 1.0, 0.0).astype(BF16)
                    for part in range(3):
                        put = total * part + rows * j + q
                        one_ref[k % 2, put : put + 16, :] = piece
            found_refs[k % 2][...] = jnp.dot(table_ref[...], one_ref[k % 2], preferred_element_type=F32)

        def select(k):
            at = jnp.broadcast_to(lists_ref[pl.ds(first + k, 1), :] & 127, (8, 256))
            valid = entry_id < counts_ref[first + k]
            sums = [jnp.zeros((8, 256), F32)] * 3
            for j in range(16):
                here = row8 == at - 8 * j
                for c in range(3):
                    piece = found_refs[k % 2][128 * c + 8 * j : 128 * c + 8 * j + 8, :]
                    sums[c] = sums[c] + jnp.where(here, piece, 0.0)
            for c in range(3):
                value = jnp.where(valid, jnp.sum(sums[c], axis=0, keepdims=True), 0.0)
                for h in range(2):
                    tab_ref[first + k, 4 * h + c : 4 * h + c + 1, :] = value[:, 128 * h : 128 * h + 128]

        masses = [jnp.zeros((8, 128), F32)] * 2
        step = rows * chips // 8
        for k in range(8):
            search(k)
            for r in range(k * step, k * step + step):
                j, inner = r // rows, r % rows
                spread = jnp.broadcast_to(node_refs[j][3, inner : inner + 1, :], (8, 128))
                for h in range(2):
                    picked = jnp.take_along_axis(spread, lane[h], axis=1, mode="promise_in_bounds")
                    masses[h] = jnp.where(row[h] == bases[j] + inner, picked, masses[h])
            if k > 0:
                select(k - 1)
        select(7)
        for k in range(8):
            for h in range(2):
                keep = entry_id[:, 128 * h : 128 * h + 128] < counts_ref[first + k]
                tab_ref[first + k, 4 * h + 3 : 4 * h + 4, :] = jnp.where(keep, masses[h][k : k + 1, :], 0.0)
        return carry

    lax.fori_loop(0, octets, gather, 0)


def build_lists(nodes, node_lists, list_counts):
    lists = node_lists.shape[0]
    deep = 3 * len(nodes) * nodes[0].shape[1]
    return pl.pallas_call(
        list_kernel,
        out_shape=jax.ShapeDtypeStruct((lists, 8, 128), F32),
        in_specs=[vspec()] * len(nodes) + [hspec(), hspec()],
        out_specs=vspec(),
        scratch_shapes=[
            VMEM((384, deep), BF16),
            VMEM(node_lists.shape, I32),
            SMEM(list_counts.shape, I32),
            VMEM((2, deep, 256), BF16),
            VMEM((384, 256), F32),
            VMEM((384, 256), F32),
            pltpu.SemaphoreType.DMA((2,)),
        ],
        compiler_params=pltpu.CompilerParams(vmem_limit_bytes=60 << 20),
        cost_estimate=pl.CostEstimate(flops=20_000_000, bytes_accessed=1_000_000, transcendentals=0),
        name="lists",
    )(*nodes, node_lists, list_counts)


def pack_kernel(req_ref, mine_ref, theirs_ref, tab_ref, reply_ref):
    tab_ref[...] = mine_ref[...] + theirs_ref[...]

    def pack(d, carry):
        for u in range(4):
            for j in range(SLOTS):
                group = jnp.maximum(req_ref[4 * d + u, j] - 1, 0)
                reply_ref[4 * d + u, j] = tab_ref[group]
        return carry

    lax.fori_loop(0, reply_ref.shape[0] // 4, pack, 0)


def row_masks():
    row = lax.broadcasted_iota(I32, (8, 128), 0)
    return row < 4, row % 4 == 3, row


def list_features(tile):
    low, last, row = row_masks()
    sq = tile * tile
    norm = pltpu.roll(sq, 1, 0) + pltpu.roll(sq, 2, 0) + pltpu.roll(sq, 3, 0)
    g = split3(jnp.where(last, norm, tile))
    ga = [pltpu.roll(v, 4, 0) for v in g]

    def pair(a, b, h):
        if h == 0:
            return jnp.where(low, g[a], ga[b])
        return jnp.where(low, ga[a], g[b])

    ones = jnp.where(row < 3, 1.0, 0.0)
    feats = jnp.concatenate(
        [
            jnp.concatenate([pair(0, 0, h), pair(0, 1, h), pair(1, 2, h), ones], axis=0)
            for h in range(2)
        ],
        axis=1,
    ).astype(BF16)
    m1, m2, m3 = pltpu.roll(tile, 7, 0), pltpu.roll(tile, 6, 0), pltpu.roll(tile, 5, 0)
    col = row % 4
    mass = jnp.where(col == 0, m3, jnp.where(col == 1, m2, m1))
    w = split3(jnp.where(last, tile, tile * mass))
    wa = [pltpu.roll(v, 4, 0) for v in w]
    zero = jnp.zeros((8, 128), F32)
    loaded = jnp.concatenate(
        [
            jnp.concatenate(
                [
                    jnp.where(low, w[0], wa[1]) if h == 0 else jnp.where(low, wa[0], w[1]),
                    jnp.where(low, w[2] if h == 0 else wa[2], zero),
                ],
                axis=0,
            )
            for h in range(2)
        ],
        axis=1,
    ).astype(BF16)
    return feats, loaded


def weights(s):
    q = lax.rsqrt(s)
    t = 1.0 / (s * q + 1.0)
    p = t + MONIC[5]
    for k in (4, 3, 2, 1, 0):
        p = p * t + MONIC[k]
    e = jnp.exp2(s * DECAY)
    return (q * q) * e * (q * p + TAIL)


def run_items(groups, blk_ref, half_ref, nact_ref, fc_ref, tab_ref, acc_ref, bufs):
    last_block = fc_ref.shape[0] - 1
    s_bufs, y_bufs = bufs

    def items(g):
        return [g * KI + k for k in range(KI)]

    def widest(g):
        n = I32(0)
        for i in items(g):
            n = jnp.maximum(n, nact_ref[jnp.minimum(blk_ref[i], last_block)])
        return n

    def two_halves(first, second):
        low, _, _ = row_masks()
        a = tab_ref[first >> 1]
        b = tab_ref[jnp.maximum(second, 0) >> 1]
        a = jnp.where((first & 1) == 1, pltpu.roll(a, 4, 0), a)
        b = jnp.where((second & 1) == 1, b, pltpu.roll(b, 4, 0))
        return jnp.where(low, a, jnp.where(second >= 0, b, 0.0))

    def prepare(g, k, width):
        i = g * KI + k
        b = jnp.minimum(blk_ref[i], last_block)
        feats, loaded = list_features(two_halves(half_ref[2 * i], half_ref[2 * i + 1]))
        y_bufs[k][...] = loaded
        wide = 128 if width == 128 else 256
        columns = jnp.transpose(fc_ref[b, :, :wide])[:width]
        s_bufs[k][:width, :] = jnp.dot(columns, feats, preferred_element_type=F32)

    def reduce(k, width):
        his, los = [], []
        for j in range(0, width, 16):
            w = weights(s_bufs[k][j : j + 16, :])
            hi = w.astype(BF16)
            his.append(hi)
            los.append((w - hi.astype(F32)).astype(BF16))
        loaded = y_bufs[k][...]
        return nt_dot(loaded, jnp.concatenate(his, axis=0)) + nt_dot(loaded, jnp.concatenate(los, axis=0))

    def by_width(n, body):
        low = -1
        for width in WIDTHS:
            @pl.when((n > low) & (n <= width))
            def _(width=width):
                body(width)

            low = width

    def step(g, carry):
        n = jnp.maximum(widest(g), widest(g + 1))

        def body(width):
            made = []
            for k in range(KI):
                made.append(reduce(k, width))
                prepare(g + 1, k, width)
            for k, i in enumerate(items(g)):
                b = blk_ref[i]
                acc_ref[b, :, :width] = acc_ref[b, :, :width] + made[k]

        by_width(n, body)
        return carry

    for k in range(KI):
        prepare(0, k, 256)
    lax.fori_loop(0, groups, step, 0)


def buffers():
    return (
        *[VMEM((256, 256), F32) for _ in range(KI)],
        *[VMEM((16, 256), BF16) for _ in range(KI)],
    )


def take_buffers(flat):
    return flat[:KI], flat[KI:]


PAD = 3 * KI


def home_kernel(
    home_ref, slot_ref, groups_ref, req_ref, nact_ref, pos_ref, bins_ref, tab_ref,
    fc_ref, key_ref, acc_ref, blk_out, half_out, n_out, blk_ref, half_ref, chosen_ref, *flat
):
    _, blocks, width = pos_ref.shape
    active = bins_ref[...] <= CUR_BIN
    tri = lax.broadcasted_iota(I32, (width, width), 0) <= lax.broadcasted_iota(I32, (width, width), 1)
    upto = jnp.dot(
        jnp.where(active, 1.0, 0.0).astype(BF16),
        jnp.where(tri, 1.0, 0.0).astype(BF16),
        preferred_element_type=F32,
    )
    key_ref[...] = jnp.where(active, upto - 1.0, -1.0).astype(I32)

    low8 = lax.broadcasted_iota(I32, (8, width), 0) < 4
    row8 = lax.broadcasted_iota(I32, (8, width), 0)
    row16 = lax.broadcasted_iota(I32, (16, width), 0)

    def compact(bb, carry):
        for u in range(4):
            b = bb * 4 + u
            key = jnp.broadcast_to(key_ref[pl.ds(b, 1), :], (16, width))
            for j in range(0, width, 16):
                chosen_ref[u, j : j + 16, :] = jnp.where(row16 == key - j, 1.0, 0.0).astype(BF16)
            pos = jnp.concatenate(
                [pos_ref[c, pl.ds(b, 1), :] * BETA for c in range(3)] + [jnp.zeros((5, width), F32)], axis=0
            )
            parts = jnp.concatenate(split3(pos), axis=0).astype(BF16)
            moved = nt_dot(parts, chosen_ref[u])
            x = (moved[0:8] + moved[8:16]) + moved[16:24]
            sq = x * x
            norm = sq[0:1] + sq[1:2] + sq[2:3] + SOFT * BETA * BETA
            n1, n2, n3 = split3(norm)
            a1, a2, a3 = split3(x * -2.0)
            unit = jnp.where(row8 == 3, 1.0, 0.0)
            a1 = a1 + unit
            r1, r2 = pltpu.roll(a1, 4, 0), pltpu.roll(a2, 4, 0)
            feats = jnp.concatenate(
                [
                    jnp.where(low8, a1, r2),
                    jnp.where(low8, a3, r1),
                    jnp.where(low8, a2, r1),
                    jnp.concatenate([n1, n2, n3, jnp.zeros((5, width), F32)], axis=0),
                ],
                axis=0,
            )
            fc_ref[b] = feats.astype(BF16)
            acc_ref[b] = jnp.zeros((16, width), F32)
        return carry

    lax.fori_loop(0, blocks // 4, compact, 0)
    acc_ref[blocks] = jnp.zeros((16, width), F32)

    def home_item(i, carry):
        inside = i < blocks
        b = jnp.minimum(i, blocks - 1)
        blk_ref[i] = jnp.where(inside, i, blocks)
        half_ref[2 * i] = 2 * home_ref[b]
        half_ref[2 * i + 1] = 2 * home_ref[b] + 1
        return carry

    lax.fori_loop(0, blocks + PAD, home_item, 0)
    run_items((blocks + KI - 1) // KI, blk_ref, half_ref, nact_ref, fc_ref, tab_ref, acc_ref, take_buffers(flat))

    most = slot_ref.shape[1] // blocks
    lists = 128 // 2

    def visits(b, n):
        for v in range(most):
            slot = slot_ref[0, v * blocks + b]
            used = jnp.where(slot >= 0, 1, 0)
            place = jnp.maximum(slot, 0)
            count = req_ref[place >> 3, lists + groups_ref[v, b]]
            blk_out[n >> 1] = b
            half_out[n] = 2 * place
            n = n + used
            blk_out[n >> 1] = b
            half_out[n] = 2 * place + 1
            n = n + jnp.where(count > 128, used, 0)
        half_out[n] = -1
        return n + (n & 1)

    end = lax.fori_loop(0, blocks, visits, I32(0)) >> 1

    def no_item(k, carry):
        blk_out[k] = blocks
        half_out[2 * k] = 0
        half_out[2 * k + 1] = -1
        return carry

    lax.fori_loop(end, end + PAD, no_item, 0)
    n_out[0] = end


def remote_kernel(n_ref, blk_ref, half_ref, nact_ref, fc_ref, tab_ref, acc_in_ref, key_ref, pos_ref, out_ref, acc_ref, *flat):
    blocks = pos_ref.shape[1]
    acc_ref[...] = acc_in_ref[...]
    run_items((n_ref[0] + KI - 1) // KI, blk_ref, half_ref, nact_ref, fc_ref, tab_ref, acc_ref, take_buffers(flat))

    def finish(bb, carry):
        for u in range(4):
            b = bb * 4 + u
            acc = acc_ref[b]
            top = acc[0:8]
            total = top + pltpu.roll(top, 4, 0) + acc[8:16]
            key = key_ref[pl.ds(b, 1), :]
            parts = []
            for h in range(2):
                at = jnp.broadcast_to(key[:, 128 * h : 128 * h + 128], (8, 128))
                lane = at & 127
                left = jnp.take_along_axis(total[:, :128], lane, axis=1, mode="promise_in_bounds")
                right = jnp.take_along_axis(total[:, 128:], lane, axis=1, mode="promise_in_bounds")
                parts.append(jnp.where(at < 128, left, right))
            back = jnp.concatenate(parts, axis=1)
            for c in range(3):
                pull = (back[c : c + 1] - pos_ref[c, pl.ds(b, 1), :] * (BETA * back[3:4])) * OUT_SCALE
                out_ref[c, pl.ds(b, 1), :] = jnp.where(key >= 0, pull, 0.0)
        return carry

    lax.fori_loop(0, blocks // 4, finish, 0)


def forces_of(positions, time_bins, home_groups, targets, target_groups, node_pos, node_mass, node_lists, list_counts):
    domains = lax.axis_size("dom")
    sharers = lax.axis_size("sub")
    blocks, most = targets.shape
    pairs = blocks * most
    width = positions.shape[2]
    lists = node_lists.shape[0]
    rows = node_mass.shape[0] // 128

    asked = (targets.T, target_groups.T, list_counts.reshape(1, lists), node_pos, node_mass.reshape(1, -1))
    req, slot, nodes = pl.pallas_call(
        request_kernel,
        out_shape=(
            jax.ShapeDtypeStruct((domains, 128), I32),
            jax.ShapeDtypeStruct((1, pairs), I32),
            jax.ShapeDtypeStruct((4, rows, 128), F32),
        ),
        in_specs=[hspec()] * 5,
        out_specs=(vspec(),) * 3,
        scratch_shapes=[*[VMEM(a.shape, a.dtype) for a in asked], pltpu.SemaphoreType.DMA((5,))],
        compiler_params=pltpu.CompilerParams(vmem_limit_bytes=60 << 20),
        name="requests",
    )(*asked)
    held = [nodes]
    for j in range(1, sharers // 2):
        held.append(lax.ppermute(nodes, "sub", [(i, (i + 2 * j) % sharers) for i in range(sharers)]))
    req = lax.all_to_all(req.reshape(domains, 1, 128), "dom", 0, 0, tiled=True)
    req = req.reshape(domains, 128)
    nact = jnp.sum((time_bins <= CUR_BIN).astype(I32), axis=1)

    mine = build_lists(held, node_lists, list_counts)
    theirs = lax.ppermute(mine, "sub", [(i, i ^ 1) for i in range(sharers)])
    tab, reply = pl.pallas_call(
        pack_kernel,
        out_shape=(
            jax.ShapeDtypeStruct((lists, 8, 128), F32),
            jax.ShapeDtypeStruct((domains, SLOTS, 8, 128), F32),
        ),
        in_specs=[sspec(), vspec(), vspec()],
        out_specs=(vspec(),) * 2,
        compiler_params=pltpu.CompilerParams(vmem_limit_bytes=60 << 20),
        name="pack",
    )(req, mine, theirs)
    reply = lax.all_to_all(reply.reshape(domains, SLOTS * 8, 128), "dom", 0, 0, tiled=True)

    positions = jnp.transpose(positions, (1, 0, 2))
    room = pairs + PAD
    fc, key, acc, blk, half, n = pl.pallas_call(
        home_kernel,
        out_shape=(
            jax.ShapeDtypeStruct((blocks, 32, width), BF16),
            jax.ShapeDtypeStruct((blocks, width), I32),
            jax.ShapeDtypeStruct((blocks + 1, 16, width), F32),
            jax.ShapeDtypeStruct((room,), I32),
            jax.ShapeDtypeStruct((2 * room,), I32),
            jax.ShapeDtypeStruct((8,), I32),
        ),
        in_specs=[sspec()] * 5 + [vspec()] * 3,
        out_specs=(vspec(),) * 3 + (sspec(),) * 3,
        scratch_shapes=[SMEM((blocks + PAD,), I32), SMEM((2 * (blocks + PAD),), I32), VMEM((4, width, width), BF16), *buffers()],
        compiler_params=pltpu.CompilerParams(vmem_limit_bytes=60 << 20),
        cost_estimate=pl.CostEstimate(flops=40_000_000, bytes_accessed=4_000_000, transcendentals=12_000_000),
        name="home_pulls",
    )(home_groups, slot, target_groups.T, req, nact, positions, time_bins, tab)

    out = pl.pallas_call(
        remote_kernel,
        out_shape=jax.ShapeDtypeStruct((3, blocks, width), F32),
        in_specs=[sspec()] * 4 + [vspec()] * 5,
        out_specs=vspec(),
        scratch_shapes=[VMEM((blocks + 1, 16, width), F32), *buffers()],
        compiler_params=pltpu.CompilerParams(vmem_limit_bytes=60 << 20),
        name="remote_pulls",
    )(n, blk, half, nact, fc, reply.reshape(domains * SLOTS, 8, 128), acc, key, positions)
    return jnp.transpose(out, (1, 0, 2))


def solution(mesh):
    return jax.shard_map(
        forces_of,
        mesh=mesh,
        in_specs=(
            P(("dom", "sub"), None, None),
            P(("dom", "sub"), None),
            P(("dom", "sub")),
            P(("dom", "sub"), None),
            P(("dom", "sub"), None),
            P(None, ("dom", "sub")),
            P(("dom", "sub")),
            P("dom", None),
            P("dom"),
        ),
        out_specs=P(("dom", "sub"), None, None),
        check_vma=False,
    )
```

profile of v0, /device:TPU:0, one launch (start us, length us, event | category | flops | bytes accessed | tf_op | source)
XLA Modules:
  0.0 110.8 jit_solution(8969467849954083251)
XLA Ops:
  0.0 1.9 %requests.1 = (s32[32,128]{1,0:T(8,128)}, s32[1,256]{1,0:T(1,128)}, f32[4,32,128]{2,1,0:T(8,128)}) custom-call(s32[4,64]{1,0:T(4,128)} %bitcast.20, s32[4,64]{1,0:T(4,128)} %bitcast.21, s32[1,64]{1,0:T(1,128)} %bitcast.23, f32[3,4096]{1,0:T(4,128)} %refs_3_.1, f32[1,4096]{1,0:T(1,128)} %bitcast.19), custom_call_target="tpu_custom_call" | custom-call | tf_op jit(solution)/shard_map/requests/pallas_call | solution.py:485
  1.9 1.1 %collective-permute-start.2 = (f32[4,32,128]{2,1,0:T(8,128)}, f32[4,32,128]{2,1,0:T(8,128)S(1)}, u32[]{:S(2)}, u32[]{:S(2)}) collective-permute-start(f32[4,32,128]{2,1,0:T(8,128)} %get-tuple-element.18.refs_0_), channel_id=1, source_target_pairs={{0,6},{1,7},{2,0},{3,1},{4,2},{5,3},{6,4},{7,5},{8,14},{9,15},{10,... | collective-permute-start | bytes 196616 | tf_op jit(solution)/shard_map/ppermute | solution.py:500
  3.0 0.8 collective-permute-start.1
  3.8 0.9 collective-permute-start
  4.7 1.7 %collective-permute-done.2.refs_3_ = f32[4,32,128]{2,1,0:T(8,128)S(1)} collective-permute-done((f32[4,32,128]{2,1,0:T(8,128)}, f32[4,32,128]{2,1,0:T(8,128)S(1)}, u32[]{:S(2)}, u32[]{:S(2)}) %collective-permute-start.2) | collective-permute-done | bytes 65568 | tf_op jit(solution)/shard_map/ppermute | solution.py:500
  6.4 0.0 copy-start.3
  6.4 2.6 %collective-permute-done.1.refs_2_ = f32[4,32,128]{2,1,0:T(8,128)S(1)} collective-permute-done((f32[4,32,128]{2,1,0:T(8,128)}, f32[4,32,128]{2,1,0:T(8,128)S(1)}, u32[]{:S(2)}, u32[]{:S(2)}) %collective-permute-start.1) | collective-permute-done | bytes 65568 | tf_op jit(solution)/shard_map/ppermute | solution.py:500
  9.0 0.0 copy-start.4
  9.0 0.7 collective-permute-done.refs_1_
  9.7 0.0 copy-done.3
  9.7 0.0 copy-done.4
  9.7 0.0 copy-start.5
  9.7 0.6 copy-done.5
  10.3 11.4 %lists.1.mine_ref = f32[64,8,128]{2,1,0:T(8,128)} custom-call(f32[4,32,128]{2,1,0:T(8,128)} %get-tuple-element.18.refs_0_, f32[4,32,128]{2,1,0:T(8,128)} %copy-done.5, f32[4,32,128]{2,1,0:T(8,128)} %copy-done.4, f32[4,32,128]{2,1,0:T(8,128)} %copy-done.3, s32[64,256]{1,0:T(8,128)} %refs_4_.1, s32[64]{0:T(128)} %refs_5_.1), custom_call_target="tpu_custom_call" | custom-call | flops 20000000 | bytes 1000000 | tf_op jit(solution)/shard_map/lists/pallas_call | solution.py:180
  21.7 0.1 collective-permute-start.3
  21.8 21.2 %all_to_all.10 = s32[32,1,128]{2,1,0:T(1,128)} all-to-all(s32[32,1,128]{2,1,0:T(1,128)} %bitcast.18), channel_id=1, replica_groups=mesh['dom'=32,'sub'=8] {'dom'}, dimensions={0} | all-to-all | bytes 32768 | tf_op jit(solution)/shard_map/all_to_all | solution.py:501
  43.1 0.0 collective-permute-done.3.theirs_ref
  43.1 0.0 copy-start.1
  43.1 0.7 copy-done.1
  43.8 2.7 %pack.1 = (f32[64,8,128]{2,1,0:T(8,128)}, f32[32,8,8,128]{3,2,1,0:T(8,128)}) custom-call(s32[32,128]{1,0:T(8,128)} %bitcast.16, f32[64,8,128]{2,1,0:T(8,128)} %lists.1.mine_ref, f32[64,8,128]{2,1,0:T(8,128)} %copy-done.1), custom_call_target="tpu_custom_call" | custom-call | tf_op jit(solution)/shard_map/pack/pallas_call | solution.py:507
  46.4 0.0 copy-start.2
  46.4 4.1 %all-to-all-start.1 = ((f32[32,64,128]{2,1,0:T(8,128)}), f32[32,64,128]{2,1,0:T(8,128)S(1)}, u32[]{:S(2)}, u32[]{:S(2)}) async-start(f32[32,64,128]{2,1,0:T(8,128)} %bitcast.13), calls=%async_computation.1 | async-start | bytes 2097152 | tf_op jit(solution)/shard_map/all_to_all | solution.py:518
  50.5 0.0 copy-done.2
  50.5 0.6 convert_reduce_fusion.nact_ref
  51.1 22.5 %home_pulls.1 = (bf16[64,32,256]{2,1,0:T(8,128)(2,1)}, s32[64,256]{1,0:T(8,128)}, f32[65,16,256]{2,1,0:T(8,128)}, s32[274]{0:T(512)}, s32[548]{0:T(1024)}, /*index=5*/s32[8]{0:T(128)}) custom-call(s32[64]{0:T(128)} %home_ref.1, s32[1,256]{1,0:T(1,128)} %get-tuple-element.16.slot_ref, s32[4,64]{1,0:T(4,128)} %bitcast.22, s32[32,128]{1,0:T(8,128)} %bitcast.17, ...), custom_call_target="tpu_custom_call" | custom-call | flops 40000000 | bytes 4000000 | tf_op jit(solution)/shard_map/home_pulls/pallas_call | solution.py:522
  73.6 5.3 %all-to-all-done.1 = f32[32,64,128]{2,1,0:T(8,128)S(1)} async-done(((f32[32,64,128]{2,1,0:T(8,128)}), f32[32,64,128]{2,1,0:T(8,128)S(1)}, u32[]{:S(2)}, u32[]{:S(2)}) %all-to-all-start.1) | async-done | bytes 1048608 | tf_op jit(solution)/shard_map/all_to_all | solution.py:518
  79.0 0.0 copy-start
  79.0 1.0 copy-done
  80.0 30.8 %remote_pulls.1 = f32[3,64,256]{2,1,0:T(8,128)} custom-call(s32[8]{0:T(128)} %get-tuple-element.20.n_ref, s32[274]{0:T(512)} %get-tuple-element.21.blk_ref, s32[548]{0:T(1024)} %get-tuple-element.22.half_ref, s32[64]{0:T(128)} %convert_reduce_fusion.nact_ref, bf16[64,32,256]{2,1,0:T(8,128)(2,1)} %get-tuple-element.23.fc_ref, f32[256,8,128]{2,1,0:T(8,128)} %bitcast.12, ...), custom_call_target="tpu_custom_call" | custom-call | tf_op jit(solution)/shard_map/remote_pulls/pallas_call | solution.py:540
Async XLA Ops:
  1.9 4.6 %collective-permute-start.2 = (f32[4,32,128]{2,1,0:T(8,128)}, f32[4,32,128]{2,1,0:T(8,128)S(1)}, u32[]{:S(2)}, u32[]{:S(2)}) collective-permute-start(f32[4,32,128]{2,1,0:T(8,128)} %get-tuple-element.18.refs_0_), channel_id=1, source_target_pairs={{0,6},{1,7},{2,0},{3,1},{4,2},{5,3},{6,4},{7,5},{8,14},{9,15},{10,... | collective-permute-start | bytes 196616 | tf_op jit(solution)/shard_map/ppermute | solution.py:500
  3.0 6.0 %collective-permute-start.1 = (f32[4,32,128]{2,1,0:T(8,128)}, f32[4,32,128]{2,1,0:T(8,128)S(1)}, u32[]{:S(2)}, u32[]{:S(2)}) collective-permute-start(f32[4,32,128]{2,1,0:T(8,128)} %get-tuple-element.18.refs_0_), channel_id=1, source_target_pairs={{0,4},{1,5},{2,6},{3,7},{4,0},{5,1},{6,2},{7,3},{8,12},{9,13},{10,... | collective-permute-start | bytes 196616 | tf_op jit(solution)/shard_map/ppermute | solution.py:500
  3.8 5.9 %collective-permute-start = (f32[4,32,128]{2,1,0:T(8,128)}, f32[4,32,128]{2,1,0:T(8,128)S(1)}, u32[]{:S(2)}, u32[]{:S(2)}) collective-permute-start(f32[4,32,128]{2,1,0:T(8,128)} %get-tuple-element.18.refs_0_), channel_id=1, source_target_pairs={{0,2},{1,3},{2,4},{3,5},{4,6},{5,7},{6,0},{7,1},{8,10},{9,11},{10,... | collective-permute-start | bytes 196616 | tf_op jit(solution)/shard_map/ppermute | solution.py:500
  6.4 3.3 %copy-start.3 = (f32[4,32,128]{2,1,0:T(8,128)}, f32[4,32,128]{2,1,0:T(8,128)S(1)}, u32[]{:S(2)}) copy-start(f32[4,32,128]{2,1,0:T(8,128)S(1)} %collective-permute-done.2.refs_3_) | copy-start | bytes 196612
  9.0 0.7 copy-start.4
  9.7 0.6 copy-start.5
  21.7 21.3 %collective-permute-start.3 = (f32[64,8,128]{2,1,0:T(8,128)}, f32[64,8,128]{2,1,0:T(8,128)S(1)}, u32[]{:S(2)}, u32[]{:S(2)}) collective-permute-start(f32[64,8,128]{2,1,0:T(8,128)} %lists.1.mine_ref), channel_id=1, source_target_pairs={{0,1},{1,0},{2,3},{3,2},{4,5},{5,4},{6,7},{7,6},{8,9},{9,8},{10,11... | collective-permute-start | bytes 786440 | tf_op jit(solution)/shard_map/ppermute | solution.py:506
  43.1 0.7 copy-start.1
  46.4 4.1 %copy-start.2 = (s32[64,256]{1,0:T(8,128)S(1)}, s32[64,256]{1,0:T(8,128)}, u32[]{:S(2)}) copy-start(s32[64,256]{1,0:T(8,128)} %bins_ref.1) | copy-start | bytes 196612
  46.4 32.5 %all-to-all-start.1 = ((f32[32,64,128]{2,1,0:T(8,128)}), f32[32,64,128]{2,1,0:T(8,128)S(1)}, u32[]{:S(2)}, u32[]{:S(2)}) async-start(f32[32,64,128]{2,1,0:T(8,128)} %bitcast.13), calls=%async_computation.1 | async-start | bytes 2097152 | tf_op jit(solution)/shard_map/all_to_all | solution.py:518
  79.0 1.0 copy-start
where the time goes:
time: 111 us
  Pallas kernels  69.3 us (62%)
  blocking collectives  21.2 us (19%)
  waiting for transfers between devices  10.3 us (9%)
  starting transfers between devices  6.96 us (6%)
  local copies, waits for them, and re-layouts  2.34 us (2%)
    pallas_call x1, Pallas kernels, forces_of(): pl.pallas_call(remote_kernel, out_shape=jax.ShapeDtypeStruct((3, blocks,...  30.8 us
    pallas_call x1, Pallas kernels, forces_of(): pl.pallas_call(home_kernel, out_shape=(jax.ShapeDtypeStruct((blocks, 32,...  22.5 us
    all_to_all x1, blocking collectives, forces_of(): req = lax.all_to_all(req.reshape(domains, 1, 128), 'dom', 0, 0, tiled=True)  21.2 us
    pallas_call x1, Pallas kernels, build_lists(): pl.pallas_call(list_kernel, out_shape=jax.ShapeDtypeStruct((lists, 8, 128...  11.4 us
    all_to_all x1, waiting for transfers between devices, forces_of(): lax.all_to_all(reply.reshape(domains, SLOTS * 8, 128), 'dom', 0, 0, tiled...  5.32 us
    ppermute x3, waiting for transfers between devices, forces_of(): lax.ppermute(nodes, 'sub', [(i, (i + 2 * j) % sharers) for i in range(sha...  4.99 us
    all_to_all x1, starting transfers between devices, forces_of(): lax.all_to_all(reply.reshape(domains, SLOTS * 8, 128), 'dom', 0, 0, tiled...  4.06 us
    ppermute x3, starting transfers between devices, forces_of(): lax.ppermute(nodes, 'sub', [(i, (i + 2 * j) % sharers) for i in range(sha...  2.81 us
  transfers between devices with their start and end apart: 5, of which 4 were waited for; matrix products, arithmetic and copies ran while one was open for 1% of the time, Pallas kernels for 20%

commit v1 on v0

--- a/solution.py
+++ b/solution.py
@@ -14,21 +14,19 @@
 BF16 = jnp.bfloat16
 I32 = jnp.int32
 
-BETA = 0.3
+SHIFT = 0.245
 POLY = (
-    0.000177460321,
-    0.334470999,
-    0.374323182,
-    0.116028516,
-    0.555240376,
-    -0.510157925,
-    0.129925288,
+    0.999994348,
+    -0.564111497,
+    0.111462021,
+    -0.00487730517,
+    -0.00155512244,
+    0.000185247258,
 )
-LEAD = POLY[6]
-MONIC = tuple(c / LEAD for c in POLY[:6])
-TAIL = 1.0 / (BETA * math.sqrt(math.pi) * LEAD)
-DECAY = -math.log2(math.e) / (4.0 * BETA * BETA)
-OUT_SCALE = BETA * BETA * LEAD
+LEAD = POLY[5]
+MONIC = tuple(c / LEAD for c in POLY[:5])
+TAIL = 1.0 / (math.sqrt(math.pi) * LEAD)
+DECAY = -0.25 * math.log2(math.e)
 
 WIDTHS = (128, 144, 160, 192, 256)
 KI = 6
@@ -68,10 +66,10 @@
 
 
 def request_kernel(*refs):
-    sources, (req_ref, slot_ref, nodes_ref), held, sems = refs[:5], refs[5:8], refs[8:13], refs[13]
+    sources, (req_ref, slot_ref, nact_ref, nodes_ref), held, sems = refs[:6], refs[6:10], refs[10:16], refs[16]
     for copy in fetch(sources, held, sems):
         copy.wait()
-    targets_ref, groups_ref, counts_ref, pos_ref, mass_ref = held
+    targets_ref, groups_ref, counts_ref, pos_ref, mass_ref, bins_ref = held
     most = targets_ref.shape[0]
     pairs = most * targets_ref.shape[1]
     domains = req_ref.shape[0]
@@ -86,6 +84,8 @@
     rank = jnp.sum(jnp.where((along == down) & earlier, 1.0, 0.0), axis=0, keepdims=True)
     slot = jnp.where(dest >= 0, dest * SLOTS + rank, -1.0)
     slot_ref[...] = slot.astype(I32)
+    active = jnp.where(bins_ref[...] <= CUR_BIN, 1.0, 0.0).astype(BF16)
+    nact_ref[...] = nt_dot(jnp.ones((16, active.shape[1]), BF16), active)[0:1].astype(I32)
     dom_id = lax.broadcasted_iota(I32, (domains, pairs), 0).astype(F32)
     asked = in_line(groups_ref) + 1.0
     by_dom = jnp.where(dom_id == dest, asked, 0.0).astype(BF16)
@@ -114,7 +114,7 @@
     bases = [lax.rem(lax.axis_index("sub") + sharers - 2 * j, sharers) * rows for j in range(chips)]
     for c in range(3):
         tall = jnp.concatenate([ref[c] for ref in node_refs], axis=0)
-        parts = split3(jnp.transpose(tall) * BETA)
+        parts = split3(jnp.transpose(tall))
         for k in range(3):
             table_ref[128 * c : 128 * c + 128, total * k : total * k + total] = parts[k].astype(BF16)
     for copy in copies:
@@ -259,9 +259,9 @@
 
 def weights(s):
     q = lax.rsqrt(s)
-    t = 1.0 / (s * q + 1.0)
-    p = t + MONIC[5]
-    for k in (4, 3, 2, 1, 0):
+    t = 1.0 / (q + SHIFT)
+    p = t + MONIC[4]
+    for k in (3, 2, 1, 0):
         p = p * t + MONIC[k]
     e = jnp.exp2(s * DECAY)
     return (q * q) * e * (q * p + TAIL)
@@ -269,16 +269,12 @@
 
 def run_items(groups, blk_ref, half_ref, nact_ref, fc_ref, tab_ref, acc_ref, bufs):
     last_block = fc_ref.shape[0] - 1
-    s_bufs, y_bufs = bufs
-
-    def items(g):
-        return [g * KI + k for k in range(KI)]
-
-    def widest(g):
-        n = I32(0)
-        for i in items(g):
-            n = jnp.maximum(n, nact_ref[jnp.minimum(blk_ref[i], last_block)])
-        return n
+    nobody = acc_ref.shape[0] - 1
+    s_bufs, y_bufs, w_buf = bufs
+    last = KI - 1
+
+    def active_in(i):
+        return nact_ref[jnp.minimum(blk_ref[i], last_block)]
 
     def two_halves(first, second):
         low, _, _ = row_masks()
@@ -288,24 +284,42 @@
         b = jnp.where((second & 1) == 1, b, pltpu.roll(b, 4, 0))
         return jnp.where(low, a, jnp.where(second >= 0, b, 0.0))
 
-    def prepare(g, k, width):
+    def prepare(g, k, par, width):
         i = g * KI + k
         b = jnp.minimum(blk_ref[i], last_block)
         feats, loaded = list_features(two_halves(half_ref[2 * i], half_ref[2 * i + 1]))
-        y_bufs[k][...] = loaded
+        y_bufs[par][k][...] = loaded
         wide = 128 if width == 128 else 256
         columns = jnp.transpose(fc_ref[b, :, :wide])[:width]
-        s_bufs[k][:width, :] = jnp.dot(columns, feats, preferred_element_type=F32)
-
-    def reduce(k, width):
-        his, los = [], []
+        s_bufs[par][k][:width, :] = jnp.dot(columns, feats, preferred_element_type=F32)
+
+    def split_weights(k, par, width):
         for j in range(0, width, 16):
-            w = weights(s_bufs[k][j : j + 16, :])
+            w = weights(s_bufs[par][k][j : j + 16, :])
             hi = w.astype(BF16)
-            his.append(hi)
-            los.append((w - hi.astype(F32)).astype(BF16))
-        loaded = y_bufs[k][...]
-        return nt_dot(loaded, jnp.concatenate(his, axis=0)) + nt_dot(loaded, jnp.concatenate(los, axis=0))
+            yield j, hi, (w - hi.astype(F32)).astype(BF16)
+
+    def reduce(k, par, width):
+        pieces = list(split_weights(k, par, width))
+        loaded = y_bufs[par][k][...]
+        hi = jnp.concatenate([p[1] for p in pieces], axis=0)
+        lo = jnp.concatenate([p[2] for p in pieces], axis=0)
+        return nt_dot(loaded, hi) + nt_dot(loaded, lo)
+
+    def leave(par, width):
+        for j, hi, lo in split_weights(last, par, width):
+            w_buf[0, j : j + 16, :] = hi
+            w_buf[1, j : j + 16, :] = lo
+
+    def left(par, width):
+        loaded = y_bufs[par][last][...]
+        return nt_dot(loaded, w_buf[0, :width, :]) + nt_dot(loaded, w_buf[1, :width, :])
+
+    def add(b, made, width):
+        acc_ref[b, :, :width] = acc_ref[b, :, :width] + made
+
+    def before(g):
+        return jnp.where(g > 0, blk_ref[jnp.maximum(g * KI - 1, 0)], nobody)
 
     def by_width(n, body):
         low = -1
@@ -316,43 +330,59 @@
 
             low = width
 
-    def step(g, carry):
-        n = jnp.maximum(widest(g), widest(g + 1))
+    def step(g, par):
+        n = nact_ref[jnp.minimum(before(g), last_block)]
+        for k in range(2 * KI):
+            n = jnp.maximum(n, active_in(g * KI + k))
 
         def body(width):
+            old = left(1 - par, width)
             made = []
             for k in range(KI):
-                made.append(reduce(k, width))
-                prepare(g + 1, k, width)
-            for k, i in enumerate(items(g)):
-                b = blk_ref[i]
-                acc_ref[b, :, :width] = acc_ref[b, :, :width] + made[k]
+                prepare(g + 1, k, 1 - par, width)
+            for k in range(KI):
+                if k < last:
+                    made.append(reduce(k, par, width))
+                else:
+                    leave(par, width)
+            add(before(g), old, width)
+            for k in range(last):
+                add(blk_ref[g * KI + k], made[k], width)
 
         by_width(n, body)
+
+    def two_steps(gg, carry):
+        step(2 * gg, 0)
+        step(2 * gg + 1, 1)
         return carry
 
+    w_buf[...] = jnp.zeros(w_buf.shape, BF16)
+    y_bufs[1][last][...] = jnp.zeros(y_bufs[1][last].shape, BF16)
     for k in range(KI):
-        prepare(0, k, 256)
-    lax.fori_loop(0, groups, step, 0)
+        prepare(0, k, 0, 256)
+    lax.fori_loop(0, (groups + 1) // 2, two_steps, 0)
+    add(before(2 * ((groups + 1) // 2)), left(1, 256), 256)
 
 
 def buffers():
     return (
-        *[VMEM((256, 256), F32) for _ in range(KI)],
-        *[VMEM((16, 256), BF16) for _ in range(KI)],
+        *[VMEM((256, 256), F32) for _ in range(2 * KI)],
+        *[VMEM((16, 256), BF16) for _ in range(2 * KI)],
+        VMEM((2, 256, 256), BF16),
     )
 
 
 def take_buffers(flat):
-    return flat[:KI], flat[KI:]
-
-
-PAD = 3 * KI
+    s, y = flat[: 2 * KI], flat[2 * KI : -1]
+    return (s[:KI], s[KI:]), (y[:KI], y[KI:]), flat[-1]
+
+
+PAD = 4 * KI
 
 
 def home_kernel(
     home_ref, slot_ref, groups_ref, req_ref, nact_ref, pos_ref, bins_ref, tab_ref,
-    fc_ref, key_ref, acc_ref, blk_out, half_out, n_out, blk_ref, half_ref, chosen_ref, *flat
+    fc_ref, key_ref, acc_ref, blk_out, half_out, n_out, blk_ref, half_ref, order_ref, chosen_ref, *flat
 ):
     _, blocks, width = pos_ref.shape
     active = bins_ref[...] <= CUR_BIN
@@ -375,13 +405,13 @@
             for j in range(0, width, 16):
                 chosen_ref[u, j : j + 16, :] = jnp.where(row16 == key - j, 1.0, 0.0).astype(BF16)
             pos = jnp.concatenate(
-                [pos_ref[c, pl.ds(b, 1), :] * BETA for c in range(3)] + [jnp.zeros((5, width), F32)], axis=0
+                [pos_ref[c, pl.ds(b, 1), :] for c in range(3)] + [jnp.zeros((5, width), F32)], axis=0
             )
             parts = jnp.concatenate(split3(pos), axis=0).astype(BF16)
             moved = nt_dot(parts, chosen_ref[u])
             x = (moved[0:8] + moved[8:16]) + moved[16:24]
             sq = x * x
-            norm = sq[0:1] + sq[1:2] + sq[2:3] + SOFT * BETA * BETA
+            norm = sq[0:1] + sq[1:2] + sq[2:3] + SOFT
             n1, n2, n3 = split3(norm)
             a1, a2, a3 = split3(x * -2.0)
             unit = jnp.where(row8 == 3, 1.0, 0.0)
@@ -417,7 +447,19 @@
     most = slot_ref.shape[1] // blocks
     lists = 128 // 2
 
-    def visits(b, n):
+    where = I32(0)
+    low = -1
+    for high in (WIDTHS[0], WIDTHS[1], WIDTHS[-1]):
+
+        def place_block(b, n, low=low, high=high):
+            order_ref[n] = b
+            return n + jnp.where((nact_ref[b] > low) & (nact_ref[b] <= high), 1, 0)
+
+        where = lax.fori_loop(0, blocks, place_block, where)
+        low = high
+
+    def visits(at, n):
+        b = order_ref[at]
         for v in range(most):
             slot = slot_ref[0, v * blocks + b]
             used = jnp.where(slot >= 0, 1, 0)
@@ -446,7 +488,7 @@
 
 def remote_kernel(n_ref, blk_ref, half_ref, nact_ref, fc_ref, tab_ref, acc_in_ref, key_ref, pos_ref, out_ref, acc_ref, *flat):
     blocks = pos_ref.shape[1]
-    acc_ref[...] = acc_in_ref[...]
+    pltpu.sync_copy(acc_in_ref, acc_ref)
     run_items((n_ref[0] + KI - 1) // KI, blk_ref, half_ref, nact_ref, fc_ref, tab_ref, acc_ref, take_buffers(flat))
 
     def finish(bb, carry):
@@ -465,7 +507,7 @@
                 parts.append(jnp.where(at < 128, left, right))
             back = jnp.concatenate(parts, axis=1)
             for c in range(3):
-                pull = (back[c : c + 1] - pos_ref[c, pl.ds(b, 1), :] * (BETA * back[3:4])) * OUT_SCALE
+                pull = (back[c : c + 1] - pos_ref[c, pl.ds(b, 1), :] * back[3:4]) * LEAD
                 out_ref[c, pl.ds(b, 1), :] = jnp.where(key >= 0, pull, 0.0)
         return carry
 
@@ -481,17 +523,18 @@
     lists = node_lists.shape[0]
     rows = node_mass.shape[0] // 128
 
-    asked = (targets.T, target_groups.T, list_counts.reshape(1, lists), node_pos, node_mass.reshape(1, -1))
-    req, slot, nodes = pl.pallas_call(
+    asked = (targets.T, target_groups.T, list_counts.reshape(1, lists), node_pos, node_mass.reshape(1, -1), time_bins)
+    req, slot, nact, nodes = pl.pallas_call(
         request_kernel,
         out_shape=(
             jax.ShapeDtypeStruct((domains, 128), I32),
             jax.ShapeDtypeStruct((1, pairs), I32),
+            jax.ShapeDtypeStruct((1, blocks), I32),
             jax.ShapeDtypeStruct((4, rows, 128), F32),
         ),
-        in_specs=[hspec()] * 5,
-        out_specs=(vspec(),) * 3,
-        scratch_shapes=[*[VMEM(a.shape, a.dtype) for a in asked], pltpu.SemaphoreType.DMA((5,))],
+        in_specs=[hspec()] * 6,
+        out_specs=(vspec(),) * 4,
+        scratch_shapes=[*[VMEM(a.shape, a.dtype) for a in asked], pltpu.SemaphoreType.DMA((6,))],
         compiler_params=pltpu.CompilerParams(vmem_limit_bytes=60 << 20),
         name="requests",
     )(*asked)
@@ -500,7 +543,7 @@
         held.append(lax.ppermute(nodes, "sub", [(i, (i + 2 * j) % sharers) for i in range(sharers)]))
     req = lax.all_to_all(req.reshape(domains, 1, 128), "dom", 0, 0, tiled=True)
     req = req.reshape(domains, 128)
-    nact = jnp.sum((time_bins <= CUR_BIN).astype(I32), axis=1)
+    nact = nact.reshape(blocks)
 
     mine = build_lists(held, node_lists, list_counts)
     theirs = lax.ppermute(mine, "sub", [(i, i ^ 1) for i in range(sharers)])
@@ -531,7 +574,7 @@
         ),
         in_specs=[sspec()] * 5 + [vspec()] * 3,
         out_specs=(vspec(),) * 3 + (sspec(),) * 3,
-        scratch_shapes=[SMEM((blocks + PAD,), I32), SMEM((2 * (blocks + PAD),), I32), VMEM((4, width, width), BF16), *buffers()],
+        scratch_shapes=[SMEM((blocks + PAD,), I32), SMEM((2 * (blocks + PAD),), I32), SMEM((blocks + 1,), I32), VMEM((4, width, width), BF16), *buffers()],
         compiler_params=pltpu.CompilerParams(vmem_limit_bytes=60 << 20),
         cost_estimate=pl.CostEstimate(flops=40_000_000, bytes_accessed=4_000_000, transcendentals=12_000_000),
         name="home_pulls",
@@ -540,7 +583,7 @@
     out = pl.pallas_call(
         remote_kernel,
         out_shape=jax.ShapeDtypeStruct((3, blocks, width), F32),
-        in_specs=[sspec()] * 4 + [vspec()] * 5,
+        in_specs=[sspec()] * 4 + [vspec(), vspec(), hspec(), vspec(), vspec()],
         out_specs=vspec(),
         scratch_shapes=[VMEM((blocks + 1, 16, width), F32), *buffers()],
         compiler_params=pltpu.CompilerParams(vmem_limit_bytes=60 << 20),

time: 111 us -> 108 us (0.973)
  Pallas kernels: 69.3 us -> 67.8 us
    pallas_call x1, Pallas kernels: 30.8 us -> 28.3 us  [forces_of(): pl.pallas_call(remote_kernel, out_shape=jax.ShapeDtypeStruct((3, blocks,...]
    unnamed x12 -> x10, local copies, waits for them, and re-layouts: 2.34 us -> 2.34 us
  transfers between devices with their start and end apart: 5 -> 5, of which waited for: 4 -> 4; matrix products, arithmetic and copies ran while one was open for 1% -> 0% of each run, Pallas kernels for 20% -> 22%
where the time goes in v1:
time: 108 us
  Pallas kernels  67.8 us (63%)
  blocking collectives  21.4 us (20%)
  waiting for transfers between devices  9.38 us (9%)
  starting transfers between devices  7.02 us (6%)
  local copies, waits for them, and re-layouts  2.34 us (2%)
    pallas_call x1, Pallas kernels, forces_of(): pl.pallas_call(remote_kernel, out_shape=jax.ShapeDtypeStruct((3, blocks,...  28.3 us
    pallas_call x1, Pallas kernels, forces_of(): pl.pallas_call(home_kernel, out_shape=(jax.ShapeDtypeStruct((blocks, 32,...  23.6 us
    all_to_all x1, blocking collectives, forces_of(): req = lax.all_to_all(req.reshape(domains, 1, 128), 'dom', 0, 0, tiled=True)  21.4 us
    pallas_call x1, Pallas kernels, build_lists(): pl.pallas_call(list_kernel, out_shape=jax.ShapeDtypeStruct((lists, 8, 128...  11.4 us
    ppermute x3, waiting for transfers between devices, forces_of(): lax.ppermute(nodes, 'sub', [(i, (i + 2 * j) % sharers) for i in range(sha...  4.99 us
    all_to_all x1, waiting for transfers between devices, forces_of(): lax.all_to_all(reply.reshape(domains, SLOTS * 8, 128), 'dom', 0, 0, tiled...  4.39 us
    all_to_all x1, starting transfers between devices, forces_of(): lax.all_to_all(reply.reshape(domains, SLOTS * 8, 128), 'dom', 0, 0, tiled...  4.11 us
    ppermute x3, starting transfers between devices, forces_of(): lax.ppermute(nodes, 'sub', [(i, (i + 2 * j) % sharers) for i in range(sha...  2.81 us
  transfers between devices with their start and end apart: 5, of which 4 were waited for; matrix products, arithmetic and copies ran while one was open for 0% of the time, Pallas kernels for 22%

profile of v1, /device:TPU:0, one launch (start us, length us, event | category | flops | bytes accessed | tf_op | source)
XLA Modules:
  0.0 108.0 jit_solution(9219248034114905576)
XLA Ops:
  0.0 1.9 %requests.1 = (s32[32,128]{1,0:T(8,128)}, s32[1,256]{1,0:T(1,128)}, s32[1,64]{1,0:T(1,128)}, f32[4,32,128]{2,1,0:T(8,128)}) custom-call(s32[4,64]{1,0:T(4,128)} %bitcast.21, s32[4,64]{1,0:T(4,128)} %bitcast.22, s32[1,64]{1,0:T(1,128)} %bitcast.24, f32[3,4096]{1,0:T(4,128)} %refs_3_.1, f32[1,4096]{1,0:T(1,128)} %bitcast.19, s32[64,256]{1,0:T(8,128)} %bins_ref.1), custom_call_target="tpu_custom_call" | custom-call | tf_op jit(solution)/shard_map/requests/pallas_call | solution.py:527
  1.9 1.1 %collective-permute-start.2 = (f32[4,32,128]{2,1,0:T(8,128)}, f32[4,32,128]{2,1,0:T(8,128)S(1)}, u32[]{:S(2)}, u32[]{:S(2)}) collective-permute-start(f32[4,32,128]{2,1,0:T(8,128)} %get-tuple-element.20.refs_0_), channel_id=1, source_target_pairs={{0,6},{1,7},{2,0},{3,1},{4,2},{5,3},{6,4},{7,5},{8,14},{9,15},{10,... | collective-permute-start | bytes 196616 | tf_op jit(solution)/shard_map/ppermute | solution.py:543
  3.1 0.8 collective-permute-start.1
  3.9 0.9 collective-permute-start
  4.8 1.7 %collective-permute-done.2.refs_3_ = f32[4,32,128]{2,1,0:T(8,128)S(1)} collective-permute-done((f32[4,32,128]{2,1,0:T(8,128)}, f32[4,32,128]{2,1,0:T(8,128)S(1)}, u32[]{:S(2)}, u32[]{:S(2)}) %collective-permute-start.2) | collective-permute-done | bytes 65568 | tf_op jit(solution)/shard_map/ppermute | solution.py:543
  6.5 0.0 copy-start.2
  6.5 2.6 %collective-permute-done.1.refs_2_ = f32[4,32,128]{2,1,0:T(8,128)S(1)} collective-permute-done((f32[4,32,128]{2,1,0:T(8,128)}, f32[4,32,128]{2,1,0:T(8,128)S(1)}, u32[]{:S(2)}, u32[]{:S(2)}) %collective-permute-start.1) | collective-permute-done | bytes 65568 | tf_op jit(solution)/shard_map/ppermute | solution.py:543
  9.1 0.0 copy-start.3
  9.1 0.7 collective-permute-done.refs_1_
  9.8 0.0 copy-done.2
  9.8 0.0 copy-done.3
  9.8 0.0 copy-start.4
  9.8 0.6 copy-done.4
  10.4 11.4 %lists.1.mine_ref = f32[64,8,128]{2,1,0:T(8,128)} custom-call(f32[4,32,128]{2,1,0:T(8,128)} %get-tuple-element.20.refs_0_, f32[4,32,128]{2,1,0:T(8,128)} %copy-done.4, f32[4,32,128]{2,1,0:T(8,128)} %copy-done.3, f32[4,32,128]{2,1,0:T(8,128)} %copy-done.2, s32[64,256]{1,0:T(8,128)} %refs_4_.1, s32[64]{0:T(128)} %refs_5_.3), custom_call_target="tpu_custom_call" | custom-call | flops 20000000 | bytes 1000000 | tf_op jit(solution)/shard_map/lists/pallas_call | solution.py:180
  21.8 0.1 collective-permute-start.3
  21.9 21.4 %all_to_all.10 = s32[32,1,128]{2,1,0:T(1,128)} all-to-all(s32[32,1,128]{2,1,0:T(1,128)} %bitcast.20), channel_id=1, replica_groups=mesh['dom'=32,'sub'=8] {'dom'}, dimensions={0} | all-to-all | bytes 32768 | tf_op jit(solution)/shard_map/all_to_all | solution.py:544
  43.3 0.0 collective-permute-done.3.theirs_ref
  43.3 0.0 copy-start.1
  43.3 0.7 copy-done.1
  44.0 2.7 %pack.1 = (f32[64,8,128]{2,1,0:T(8,128)}, f32[32,8,8,128]{3,2,1,0:T(8,128)}) custom-call(s32[32,128]{1,0:T(8,128)} %bitcast.17, f32[64,8,128]{2,1,0:T(8,128)} %lists.1.mine_ref, f32[64,8,128]{2,1,0:T(8,128)} %copy-done.1), custom_call_target="tpu_custom_call" | custom-call | tf_op jit(solution)/shard_map/pack/pallas_call | solution.py:550
  46.6 4.1 %all-to-all-start.1 = ((f32[32,64,128]{2,1,0:T(8,128)}), f32[32,64,128]{2,1,0:T(8,128)S(1)}, u32[]{:S(2)}, u32[]{:S(2)}) async-start(f32[32,64,128]{2,1,0:T(8,128)} %bitcast.14), calls=%async_computation.1 | async-start | bytes 2097152 | tf_op jit(solution)/shard_map/all_to_all | solution.py:561
  50.8 23.6 %home_pulls.1 = (bf16[64,32,256]{2,1,0:T(8,128)(2,1)}, s32[64,256]{1,0:T(8,128)}, f32[65,16,256]{2,1,0:T(8,128)}, s32[280]{0:T(512)}, s32[560]{0:T(1024)}, /*index=5*/s32[8]{0:T(128)}) custom-call(s32[64]{0:T(128)} %home_ref.1, s32[1,256]{1,0:T(1,128)} %get-tuple-element.17.slot_ref, s32[4,64]{1,0:T(4,128)} %bitcast.23, s32[32,128]{1,0:T(8,128)} %bitcast.18, ...), custom_call_target="tpu_custom_call" | custom-call | flops 40000000 | bytes 4000000 | tf_op jit(solution)/shard_map/home_pulls/pallas_call | solution.py:565
  74.3 4.4 %all-to-all-done.1 = f32[32,64,128]{2,1,0:T(8,128)S(1)} async-done(((f32[32,64,128]{2,1,0:T(8,128)}), f32[32,64,128]{2,1,0:T(8,128)S(1)}, u32[]{:S(2)}, u32[]{:S(2)}) %all-to-all-start.1) | async-done | bytes 1048608 | tf_op jit(solution)/shard_map/all_to_all | solution.py:561
  78.7 0.0 copy-start
  78.7 1.0 copy-done
  79.7 28.3 %remote_pulls.1 = f32[3,64,256]{2,1,0:T(8,128)} custom-call(s32[8]{0:T(128)} %get-tuple-element.22.n_ref, s32[280]{0:T(512)} %get-tuple-element.23.blk_ref, s32[560]{0:T(1024)} %get-tuple-element.24.half_ref, s32[64]{0:T(128)} %bitcast.26, bf16[64,32,256]{2,1,0:T(8,128)(2,1)} %get-tuple-element.25.fc_ref, f32[256,8,128]{2,1,0:T(8,128)} %bitcast.13, ...), custom_call_target="tpu_custom_call" | custom-call | tf_op jit(solution)/shard_map/remote_pulls/pallas_call | solution.py:583
Async XLA Ops:
  1.9 4.6 %collective-permute-start.2 = (f32[4,32,128]{2,1,0:T(8,128)}, f32[4,32,128]{2,1,0:T(8,128)S(1)}, u32[]{:S(2)}, u32[]{:S(2)}) collective-permute-start(f32[4,32,128]{2,1,0:T(8,128)} %get-tuple-element.20.refs_0_), channel_id=1, source_target_pairs={{0,6},{1,7},{2,0},{3,1},{4,2},{5,3},{6,4},{7,5},{8,14},{9,15},{10,... | collective-permute-start | bytes 196616 | tf_op jit(solution)/shard_map/ppermute | solution.py:543
  3.1 6.0 %collective-permute-start.1 = (f32[4,32,128]{2,1,0:T(8,128)}, f32[4,32,128]{2,1,0:T(8,128)S(1)}, u32[]{:S(2)}, u32[]{:S(2)}) collective-permute-start(f32[4,32,128]{2,1,0:T(8,128)} %get-tuple-element.20.refs_0_), channel_id=1, source_target_pairs={{0,4},{1,5},{2,6},{3,7},{4,0},{5,1},{6,2},{7,3},{8,12},{9,13},{10,... | collective-permute-start | bytes 196616 | tf_op jit(solution)/shard_map/ppermute | solution.py:543
  3.9 5.9 %collective-permute-start = (f32[4,32,128]{2,1,0:T(8,128)}, f32[4,32,128]{2,1,0:T(8,128)S(1)}, u32[]{:S(2)}, u32[]{:S(2)}) collective-permute-start(f32[4,32,128]{2,1,0:T(8,128)} %get-tuple-element.20.refs_0_), channel_id=1, source_target_pairs={{0,2},{1,3},{2,4},{3,5},{4,6},{5,7},{6,0},{7,1},{8,10},{9,11},{10,... | collective-permute-start | bytes 196616 | tf_op jit(solution)/shard_map/ppermute | solution.py:543
  6.5 3.3 %copy-start.2 = (f32[4,32,128]{2,1,0:T(8,128)}, f32[4,32,128]{2,1,0:T(8,128)S(1)}, u32[]{:S(2)}) copy-start(f32[4,32,128]{2,1,0:T(8,128)S(1)} %collective-permute-done.2.refs_3_) | copy-start | bytes 196612
  9.1 0.7 copy-start.3
  9.8 0.6 copy-start.4
  21.8 21.5 %collective-permute-start.3 = (f32[64,8,128]{2,1,0:T(8,128)}, f32[64,8,128]{2,1,0:T(8,128)S(1)}, u32[]{:S(2)}, u32[]{:S(2)}) collective-permute-start(f32[64,8,128]{2,1,0:T(8,128)} %lists.1.mine_ref), channel_id=1, source_target_pairs={{0,1},{1,0},{2,3},{3,2},{4,5},{5,4},{6,7},{7,6},{8,9},{9,8},{10,11... | collective-permute-start | bytes 786440 | tf_op jit(solution)/shard_map/ppermute | solution.py:549
  43.3 0.7 copy-start.1
  46.6 32.1 %all-to-all-start.1 = ((f32[32,64,128]{2,1,0:T(8,128)}), f32[32,64,128]{2,1,0:T(8,128)S(1)}, u32[]{:S(2)}, u32[]{:S(2)}) async-start(f32[32,64,128]{2,1,0:T(8,128)} %bitcast.14), calls=%async_computation.1 | async-start | bytes 2097152 | tf_op jit(solution)/shard_map/all_to_all | solution.py:561
  78.7 1.0 copy-start

commit v2 on v1

--- a/solution.py
+++ b/solution.py
@@ -112,83 +112,69 @@
     copies = fetch((lists_hbm, counts_hbm), (lists_ref, counts_ref), sems)
     sharers = lax.axis_size("sub")
     bases = [lax.rem(lax.axis_index("sub") + sharers - 2 * j, sharers) * rows for j in range(chips)]
-    for c in range(3):
-        tall = jnp.concatenate([ref[c] for ref in node_refs], axis=0)
-        parts = split3(jnp.transpose(tall))
-        for k in range(3):
-            table_ref[128 * c : 128 * c + 128, total * k : total * k + total] = parts[k].astype(BF16)
+    for c in range(4):
+        tall = jnp.transpose(jnp.concatenate([ref[c] for ref in node_refs], axis=0))
+        high = tall.astype(BF16)
+        table_ref[128 * c : 128 * c + 128, :total] = high
+        table_ref[128 * c : 128 * c + 128, total:] = (tall - high.astype(F32)).astype(BF16)
     for copy in copies:
         copy.wait()
     row16 = lax.broadcasted_iota(I32, (16, 256), 0)
     row8 = lax.broadcasted_iota(I32, (8, 256), 0)
     entry_id = lax.broadcasted_iota(I32, (1, 256), 1)
 
+    def search(one, k):
+        at = jnp.broadcast_to(lists_ref[pl.ds(one, 1), :] >> 7, (16, 256))
+        for j in range(chips):
+            for q in range(0, rows, 16):
+                piece = jnp.where(row16 == at - (bases[j] + q), 1.0, 0.0).astype(BF16)
+                for part in range(2):
+                    put = total * part + rows * j + q
+                    one_ref[k % 2, put : put + 16, :] = piece
+        found_refs[k % 2][...] = jnp.dot(table_ref[...], one_ref[k % 2], preferred_element_type=F32)
+
+    def select(one, k):
+        at = jnp.broadcast_to(lists_ref[pl.ds(one, 1), :] & 127, (8, 256))
+        valid = entry_id < counts_ref[one]
+        sums = [jnp.zeros((8, 256), F32)] * 4
+        for j in range(16):
+            here = row8 == at - 8 * j
+            for c in range(4):
+                piece = found_refs[k % 2][128 * c + 8 * j : 128 * c + 8 * j + 8, :]
+                sums[c] = sums[c] + jnp.where(here, piece, 0.0)
+        for c in range(4):
+            value = jnp.where(valid, jnp.sum(sums[c], axis=0, keepdims=True), 0.0)
+            for h in range(2):
+                tab_ref[one, 4 * h + c : 4 * h + c + 1, :] = value[:, 128 * h : 128 * h + 128]
+
+    found_refs[1][...] = jnp.zeros(found_refs[1].shape, F32)
+
     def gather(i, carry):
-        first = pl.multiple_of(i * 8, 8)
-        lane = [lists_ref[pl.ds(first, 8), 128 * h : 128 * h + 128] & 127 for h in range(2)]
-        row = [lists_ref[pl.ds(first, 8), 128 * h : 128 * h + 128] >> 7 for h in range(2)]
-
-        def search(k):
-            at = jnp.broadcast_to(lists_ref[pl.ds(first + k, 1), :] >> 7, (16, 256))
-            for j in range(chips):
-                for q in range(0, rows, 16):
-                    piece = jnp.where(row16 == at - (bases[j] + q), 1.0, 0.0).astype(BF16)
-                    for part in range(3):
-                        put = total * part + rows * j + q
-                        one_ref[k % 2, put : put + 16, :] = piece
-            found_refs[k % 2][...] = jnp.dot(table_ref[...], one_ref[k % 2], preferred_element_type=F32)
-
-        def select(k):
-            at = jnp.broadcast_to(lists_ref[pl.ds(first + k, 1), :] & 127, (8, 256))
-            valid = entry_id < counts_ref[first + k]
-            sums = [jnp.zeros((8, 256), F32)] * 3
-            for j in range(16):
-                here = row8 == at - 8 * j
-                for c in range(3):
-                    piece = found_refs[k % 2][128 * c + 8 * j : 128 * c + 8 * j + 8, :]
-                    sums[c] = sums[c] + jnp.where(here, piece, 0.0)
-            for c in range(3):
-                value = jnp.where(valid, jnp.sum(sums[c], axis=0, keepdims=True), 0.0)
-                for h in range(2):
-                    tab_ref[first + k, 4 * h + c : 4 * h + c + 1, :] = value[:, 128 * h : 128 * h + 128]
-
-        masses = [jnp.zeros((8, 128), F32)] * 2
-        step = rows * chips // 8
+        first = i * 8
         for k in range(8):
-            search(k)
-            for r in range(k * step, k * step + step):
-                j, inner = r // rows, r % rows
-                spread = jnp.broadcast_to(node_refs[j][3, inner : inner + 1, :], (8, 128))
-                for h in range(2):
-                    picked = jnp.take_along_axis(spread, lane[h], axis=1, mode="promise_in_bounds")
-                    masses[h] = jnp.where(row[h] == bases[j] + inner, picked, masses[h])
-            if k > 0:
-                select(k - 1)
-        select(7)
-        for k in range(8):
-            for h in range(2):
-                keep = entry_id[:, 128 * h : 128 * h + 128] < counts_ref[first + k]
-                tab_ref[first + k, 4 * h + 3 : 4 * h + 4, :] = jnp.where(keep, masses[h][k : k + 1, :], 0.0)
+            search(first + k, k)
+            select(jnp.maximum(first + k - 1, 0), k + 1)
         return carry
 
     lax.fori_loop(0, octets, gather, 0)
+    select(8 * octets - 1, 1)
 
 
 def build_lists(nodes, node_lists, list_counts):
     lists = node_lists.shape[0]
-    deep = 3 * len(nodes) * nodes[0].shape[1]
+    deep = 2 * len(nodes) * nodes[0].shape[1]
     return pl.pallas_call(
         list_kernel,
         out_shape=jax.ShapeDtypeStruct((lists, 8, 128), F32),
         in_specs=[vspec()] * len(nodes) + [hspec(), hspec()],
         out_specs=vspec(),
         scratch_shapes=[
-            VMEM((384, deep), BF16),
+            VMEM((512, deep), BF16),
             VMEM(node_lists.shape, I32),
             SMEM(list_counts.shape, I32),
             VMEM((2, deep, 256), BF16),
-            VMEM((384, 256), F32),
-            VMEM((384, 256), F32),
+            VMEM((512, 256), F32),
+            VMEM((512, 256), F32),
             pltpu.SemaphoreType.DMA((2,)),
         ],
         compiler_params=pltpu.CompilerParams(vmem_limit_bytes=60 << 20),
@@ -267,7 +253,7 @@
     return (q * q) * e * (q * p + TAIL)
 
 
-def run_items(groups, blk_ref, half_ref, nact_ref, fc_ref, tab_ref, acc_ref, bufs):
+def run_items(groups, blk_ref, half_ref, nact_ref, fc_ref, tab_ref, acc_ref, bufs, ready=None):
     last_block = fc_ref.shape[0] - 1
     nobody = acc_ref.shape[0] - 1
     s_bufs, y_bufs, w_buf = bufs
@@ -360,6 +346,8 @@
     y_bufs[1][last][...] = jnp.zeros(y_bufs[1][last].shape, BF16)
     for k in range(KI):
         prepare(0, k, 0, 256)
+    if ready is not None:
+        ready()
     lax.fori_loop(0, (groups + 1) // 2, two_steps, 0)
     add(before(2 * ((groups + 1) // 2)), left(1, 256), 256)
 
@@ -486,10 +474,21 @@
     n_out[0] = end
 
 
-def remote_kernel(n_ref, blk_ref, half_ref, nact_ref, fc_ref, tab_ref, acc_in_ref, key_ref, pos_ref, out_ref, acc_ref, *flat):
+def remote_kernel(n_ref, blk_ref, half_ref, nact_ref, fc_ref, tab_ref, acc_in_ref, key_ref, pos_ref, out_ref, acc_ref, sem, *flat):
     blocks = pos_ref.shape[1]
-    pltpu.sync_copy(acc_in_ref, acc_ref)
-    run_items((n_ref[0] + KI - 1) // KI, blk_ref, half_ref, nact_ref, fc_ref, tab_ref, acc_ref, take_buffers(flat))
+    copy = pltpu.make_async_copy(acc_in_ref, acc_ref, sem)
+    copy.start()
+    run_items(
+        (n_ref[0] + KI - 1) // KI,
+        blk_ref,
+        half_ref,
+        nact_ref,
+        fc_ref,
+        tab_ref,
+        acc_ref,
+        take_buffers(flat),
+        copy.wait,
+    )
 
     def finish(bb, carry):
         for u in range(4):
@@ -575,7 +574,7 @@
         in_specs=[sspec()] * 5 + [vspec()] * 3,
         out_specs=(vspec(),) * 3 + (sspec(),) * 3,
         scratch_shapes=[SMEM((blocks + PAD,), I32), SMEM((2 * (blocks + PAD),), I32), SMEM((blocks + 1,), I32), VMEM((4, width, width), BF16), *buffers()],
-        compiler_params=pltpu.CompilerParams(vmem_limit_bytes=60 << 20),
+        compiler_params=pltpu.CompilerParams(vmem_limit_bytes=65136 << 10),
         cost_estimate=pl.CostEstimate(flops=40_000_000, bytes_accessed=4_000_000, transcendentals=12_000_000),
         name="home_pulls",
     )(home_groups, slot, target_groups.T, req, nact, positions, time_bins, tab)
@@ -585,7 +584,7 @@
         out_shape=jax.ShapeDtypeStruct((3, blocks, width), F32),
         in_specs=[sspec()] * 4 + [vspec(), vspec(), hspec(), vspec(), vspec()],
         out_specs=vspec(),
-        scratch_shapes=[VMEM((blocks + 1, 16, width), F32), *buffers()],
+        scratch_shapes=[VMEM((blocks + 1, 16, width), F32), pltpu.SemaphoreType.DMA, *buffers()],
         compiler_params=pltpu.CompilerParams(vmem_limit_bytes=60 << 20),
         name="remote_pulls",
     )(n, blk, half, nact, fc, reply.reshape(domains * SLOTS, 8, 128), acc, key, positions)

time: 108 us -> 106 us (0.981)
  Pallas kernels: 67.8 us -> 65.1 us
    pallas_call x1, Pallas kernels: 11.4 us -> 9.26 us  [build_lists(): pl.pallas_call(list_kernel, out_shape=jax.ShapeDtypeStruct((lists, 8, 128...]
    unnamed x10 -> x8, local copies, waits for them, and re-layouts: 2.34 us -> 1.35 us
where the time goes in v2:
time: 106 us; the launch traced here: 105 us
  Pallas kernels  65.1 us (61%)
  blocking collectives  21.3 us (20%)
  waiting for transfers between devices  9.65 us (9%)
  starting transfers between devices  7.75 us (7%)
  local copies, waits for them, and re-layouts  1.35 us (1%)
    pallas_call x1, Pallas kernels, forces_of(): pl.pallas_call(remote_kernel, out_shape=jax.ShapeDtypeStruct((3, blocks,...  27.7 us
    pallas_call x1, Pallas kernels, forces_of(): pl.pallas_call(home_kernel, out_shape=(jax.ShapeDtypeStruct((blocks, 32,...  23.6 us
    all_to_all x1, blocking collectives, forces_of(): req = lax.all_to_all(req.reshape(domains, 1, 128), 'dom', 0, 0, tiled=True)  21.3 us
    pallas_call x1, Pallas kernels, build_lists(): pl.pallas_call(list_kernel, out_shape=jax.ShapeDtypeStruct((lists, 8, 128...  9.26 us
    ppermute x3, waiting for transfers between devices, forces_of(): lax.ppermute(nodes, 'sub', [(i, (i + 2 * j) % sharers) for i in range(sha...  4.99 us
    all_to_all x1, starting transfers between devices, forces_of(): lax.all_to_all(reply.reshape(domains, SLOTS * 8, 128), 'dom', 0, 0, tiled...  4.85 us
    all_to_all x1, waiting for transfers between devices, forces_of(): lax.all_to_all(reply.reshape(domains, SLOTS * 8, 128), 'dom', 0, 0, tiled...  4.65 us
    ppermute x3, starting transfers between devices, forces_of(): lax.ppermute(nodes, 'sub', [(i, (i + 2 * j) % sharers) for i in range(sha...  2.81 us
  transfers between devices with their start and end apart: 5, of which 4 were waited for; matrix products, arithmetic and copies ran while one was open for 0% of the time, Pallas kernels for 22%

profile of v2, /device:TPU:0, one launch (start us, length us, event | category | flops | bytes accessed | tf_op | source)
XLA Modules:
  0.0 105.3 jit_solution(15231753149817619643)
XLA Ops:
  0.0 1.9 %requests.1 = (s32[32,128]{1,0:T(8,128)}, s32[1,256]{1,0:T(1,128)}, s32[1,64]{1,0:T(1,128)}, f32[4,32,128]{2,1,0:T(8,128)}) custom-call(s32[4,64]{1,0:T(4,128)} %bitcast.20, s32[4,64]{1,0:T(4,128)} %bitcast.21, s32[1,64]{1,0:T(1,128)} %bitcast.23, f32[3,4096]{1,0:T(4,128)} %refs_3_.1, f32[1,4096]{1,0:T(1,128)} %bitcast.18, s32[64,256]{1,0:T(8,128)} %bins_ref.1), custom_call_target="tpu_custom_call" | custom-call | tf_op jit(solution)/shard_map/requests/pallas_call | solution.py:526
  1.9 1.1 %collective-permute-start.2 = (f32[4,32,128]{2,1,0:T(8,128)}, f32[4,32,128]{2,1,0:T(8,128)S(1)}, u32[]{:S(2)}, u32[]{:S(2)}) collective-permute-start(f32[4,32,128]{2,1,0:T(8,128)} %get-tuple-element.20.refs_0_), channel_id=1, source_target_pairs={{0,6},{1,7},{2,0},{3,1},{4,2},{5,3},{6,4},{7,5},{8,14},{9,15},{10,... | collective-permute-start | bytes 196616 | tf_op jit(solution)/shard_map/ppermute | solution.py:542
  3.1 0.8 collective-permute-start.1
  3.9 0.9 collective-permute-start
  4.8 1.7 %collective-permute-done.2.refs_3_ = f32[4,32,128]{2,1,0:T(8,128)S(1)} collective-permute-done((f32[4,32,128]{2,1,0:T(8,128)}, f32[4,32,128]{2,1,0:T(8,128)S(1)}, u32[]{:S(2)}, u32[]{:S(2)}) %collective-permute-start.2) | collective-permute-done | bytes 65568 | tf_op jit(solution)/shard_map/ppermute | solution.py:542
  6.5 0.0 copy-start.1
  6.5 2.6 %collective-permute-done.1.refs_2_ = f32[4,32,128]{2,1,0:T(8,128)S(1)} collective-permute-done((f32[4,32,128]{2,1,0:T(8,128)}, f32[4,32,128]{2,1,0:T(8,128)S(1)}, u32[]{:S(2)}, u32[]{:S(2)}) %collective-permute-start.1) | collective-permute-done | bytes 65568 | tf_op jit(solution)/shard_map/ppermute | solution.py:542
  9.1 0.0 copy-start.2
  9.1 0.7 collective-permute-done.refs_1_
  9.8 0.0 copy-done.1
  9.8 0.0 copy-done.2
  9.8 0.0 copy-start.3
  9.8 0.6 copy-done.3
  10.4 9.3 %lists.1.mine_ref = f32[64,8,128]{2,1,0:T(8,128)} custom-call(f32[4,32,128]{2,1,0:T(8,128)} %get-tuple-element.20.refs_0_, f32[4,32,128]{2,1,0:T(8,128)} %copy-done.3, f32[4,32,128]{2,1,0:T(8,128)} %copy-done.2, f32[4,32,128]{2,1,0:T(8,128)} %copy-done.1, s32[64,256]{1,0:T(8,128)} %refs_4_.1, s32[64]{0:T(128)} %refs_5_.3), custom_call_target="tpu_custom_call" | custom-call | flops 20000000 | bytes 1000000 | tf_op jit(solution)/shard_map/lists/pallas_call | solution.py:166
  19.7 0.1 collective-permute-start.3
  19.8 21.3 %all_to_all.10 = s32[32,1,128]{2,1,0:T(1,128)} all-to-all(s32[32,1,128]{2,1,0:T(1,128)} %bitcast.19), channel_id=1, replica_groups=mesh['dom'=32,'sub'=8] {'dom'}, dimensions={0} | all-to-all | bytes 32768 | tf_op jit(solution)/shard_map/all_to_all | solution.py:543
  41.0 0.0 collective-permute-done.3.theirs_ref
  41.0 0.0 copy-start
  41.0 0.7 copy-done
  41.7 2.7 %pack.1 = (f32[64,8,128]{2,1,0:T(8,128)}, f32[32,8,8,128]{3,2,1,0:T(8,128)}) custom-call(s32[32,128]{1,0:T(8,128)} %bitcast.16, f32[64,8,128]{2,1,0:T(8,128)} %lists.1.mine_ref, f32[64,8,128]{2,1,0:T(8,128)} %copy-done), custom_call_target="tpu_custom_call" | custom-call | tf_op jit(solution)/shard_map/pack/pallas_call | solution.py:549
  44.4 4.8 %all-to-all-start.1 = ((f32[32,64,128]{2,1,0:T(8,128)}), f32[32,64,128]{2,1,0:T(8,128)}, u32[]{:S(2)}, u32[]{:S(2)}) async-start(f32[32,64,128]{2,1,0:T(8,128)} %bitcast.13), calls=%async_computation.1 | async-start | bytes 2097152 | tf_op jit(solution)/shard_map/all_to_all | solution.py:560
  49.3 23.6 %home_pulls.1 = (bf16[64,32,256]{2,1,0:T(8,128)(2,1)}, s32[64,256]{1,0:T(8,128)}, f32[65,16,256]{2,1,0:T(8,128)}, s32[280]{0:T(512)}, s32[560]{0:T(1024)}, /*index=5*/s32[8]{0:T(128)}) custom-call(s32[64]{0:T(128)} %home_ref.1, s32[1,256]{1,0:T(1,128)} %get-tuple-element.17.slot_ref, s32[4,64]{1,0:T(4,128)} %bitcast.22, s32[32,128]{1,0:T(8,128)} %bitcast.17, ...), custom_call_target="tpu_custom_call" | custom-call | flops 40000000 | bytes 4000000 | tf_op jit(solution)/shard_map/home_pulls/pallas_call | solution.py:564
  72.8 4.7 %all-to-all-done.1 = f32[32,64,128]{2,1,0:T(8,128)} async-done(((f32[32,64,128]{2,1,0:T(8,128)}), f32[32,64,128]{2,1,0:T(8,128)}, u32[]{:S(2)}, u32[]{:S(2)}) %all-to-all-start.1) | async-done | bytes 1048608 | tf_op jit(solution)/shard_map/all_to_all | solution.py:560
  77.5 27.7 %remote_pulls.1 = f32[3,64,256]{2,1,0:T(8,128)} custom-call(s32[8]{0:T(128)} %get-tuple-element.22.n_ref, s32[280]{0:T(512)} %get-tuple-element.23.blk_ref, s32[560]{0:T(1024)} %get-tuple-element.24.half_ref, s32[64]{0:T(128)} %bitcast.25, bf16[64,32,256]{2,1,0:T(8,128)(2,1)} %get-tuple-element.25.fc_ref, f32[256,8,128]{2,1,0:T(8,128)} %bitcast.10.tab_ref, ...), custom_call_target="tpu_custom_call" | custom-call | tf_op jit(solution)/shard_map/remote_pulls/pallas_call | solution.py:582
Async XLA Ops:
  1.9 4.6 %collective-permute-start.2 = (f32[4,32,128]{2,1,0:T(8,128)}, f32[4,32,128]{2,1,0:T(8,128)S(1)}, u32[]{:S(2)}, u32[]{:S(2)}) collective-permute-start(f32[4,32,128]{2,1,0:T(8,128)} %get-tuple-element.20.refs_0_), channel_id=1, source_target_pairs={{0,6},{1,7},{2,0},{3,1},{4,2},{5,3},{6,4},{7,5},{8,14},{9,15},{10,... | collective-permute-start | bytes 196616 | tf_op jit(solution)/shard_map/ppermute | solution.py:542
  3.1 6.0 %collective-permute-start.1 = (f32[4,32,128]{2,1,0:T(8,128)}, f32[4,32,128]{2,1,0:T(8,128)S(1)}, u32[]{:S(2)}, u32[]{:S(2)}) collective-permute-start(f32[4,32,128]{2,1,0:T(8,128)} %get-tuple-element.20.refs_0_), channel_id=1, source_target_pairs={{0,4},{1,5},{2,6},{3,7},{4,0},{5,1},{6,2},{7,3},{8,12},{9,13},{10,... | collective-permute-start | bytes 196616 | tf_op jit(solution)/shard_map/ppermute | solution.py:542
  3.9 5.9 %collective-permute-start = (f32[4,32,128]{2,1,0:T(8,128)}, f32[4,32,128]{2,1,0:T(8,128)S(1)}, u32[]{:S(2)}, u32[]{:S(2)}) collective-permute-start(f32[4,32,128]{2,1,0:T(8,128)} %get-tuple-element.20.refs_0_), channel_id=1, source_target_pairs={{0,2},{1,3},{2,4},{3,5},{4,6},{5,7},{6,0},{7,1},{8,10},{9,11},{10,... | collective-permute-start | bytes 196616 | tf_op jit(solution)/shard_map/ppermute | solution.py:542
  6.5 3.3 %copy-start.1 = (f32[4,32,128]{2,1,0:T(8,128)}, f32[4,32,128]{2,1,0:T(8,128)S(1)}, u32[]{:S(2)}) copy-start(f32[4,32,128]{2,1,0:T(8,128)S(1)} %collective-permute-done.2.refs_3_) | copy-start | bytes 196612
  9.1 0.7 copy-start.2
  9.8 0.6 copy-start.3
  19.7 21.4 %collective-permute-start.3 = (f32[64,8,128]{2,1,0:T(8,128)}, f32[64,8,128]{2,1,0:T(8,128)S(1)}, u32[]{:S(2)}, u32[]{:S(2)}) collective-permute-start(f32[64,8,128]{2,1,0:T(8,128)} %lists.1.mine_ref), channel_id=1, source_target_pairs={{0,1},{1,0},{2,3},{3,2},{4,5},{5,4},{6,7},{7,6},{8,9},{9,8},{10,11... | collective-permute-start | bytes 786440 | tf_op jit(solution)/shard_map/ppermute | solution.py:548
  41.0 0.7 copy-start
  44.4 33.1 %all-to-all-start.1 = ((f32[32,64,128]{2,1,0:T(8,128)}), f32[32,64,128]{2,1,0:T(8,128)}, u32[]{:S(2)}, u32[]{:S(2)}) async-start(f32[32,64,128]{2,1,0:T(8,128)} %bitcast.13), calls=%async_computation.1 | async-start | bytes 2097152 | tf_op jit(solution)/shard_map/all_to_all | solution.py:560

commit v3 on v2

--- a/solution.py
+++ b/solution.py
@@ -28,8 +28,8 @@
 TAIL = 1.0 / (math.sqrt(math.pi) * LEAD)
 DECAY = -0.25 * math.log2(math.e)
 
-WIDTHS = (128, 144, 160, 192, 256)
-KI = 6
+WIDTHS = (128, 144, 160, 256)
+KI = 8
 VMEM = pltpu.VMEM
 SMEM = pltpu.SMEM
 SLOTS = 8
@@ -183,17 +183,22 @@
     )(*nodes, node_lists, list_counts)
 
 
-def pack_kernel(req_ref, mine_ref, theirs_ref, tab_ref, reply_ref):
-    tab_ref[...] = mine_ref[...] + theirs_ref[...]
-
-    def pack(d, carry):
-        for u in range(4):
+def pack_kernel(req_ref, mine_ref, theirs_ref, reply_hbm, reply_ref, sems):
+    each = reply_ref.shape[0] // sems.shape[0]
+
+    def chunk(d):
+        return pltpu.make_async_copy(
+            reply_ref.at[pl.ds(each * d, each)], reply_hbm.at[pl.ds(each * d, each)], sems.at[d]
+        )
+
+    for d in range(sems.shape[0]):
+        for u in range(each):
             for j in range(SLOTS):
-                group = jnp.maximum(req_ref[4 * d + u, j] - 1, 0)
-                reply_ref[4 * d + u, j] = tab_ref[group]
-        return carry
-
-    lax.fori_loop(0, reply_ref.shape[0] // 4, pack, 0)
+                group = jnp.maximum(req_ref[each * d + u, j] - 1, 0)
+                reply_ref[each * d + u, j] = mine_ref[group] + theirs_ref[group]
+        chunk(d).start()
+    for d in range(sems.shape[0]):
+        chunk(d).wait()
 
 
 def row_masks():
@@ -253,7 +258,7 @@
     return (q * q) * e * (q * p + TAIL)
 
 
-def run_items(groups, blk_ref, half_ref, nact_ref, fc_ref, tab_ref, acc_ref, bufs, ready=None):
+def run_items(groups, blk_ref, half_ref, nact_ref, fc_ref, list_tile, acc_ref, bufs, ready=None):
     last_block = fc_ref.shape[0] - 1
     nobody = acc_ref.shape[0] - 1
     s_bufs, y_bufs, w_buf = bufs
@@ -264,8 +269,8 @@
 
     def two_halves(first, second):
         low, _, _ = row_masks()
-        a = tab_ref[first >> 1]
-        b = tab_ref[jnp.maximum(second, 0) >> 1]
+        a = list_tile(first >> 1)
+        b = list_tile(jnp.maximum(second, 0) >> 1)
         a = jnp.where((first & 1) == 1, pltpu.roll(a, 4, 0), a)
         b = jnp.where((second & 1) == 1, b, pltpu.roll(b, 4, 0))
         return jnp.where(low, a, jnp.where(second >= 0, b, 0.0))
@@ -369,7 +374,7 @@
 
 
 def home_kernel(
-    home_ref, slot_ref, groups_ref, req_ref, nact_ref, pos_ref, bins_ref, tab_ref,
+    home_ref, slot_ref, groups_ref, req_ref, nact_ref, pos_ref, bins_ref, mine_ref, theirs_ref,
     fc_ref, key_ref, acc_ref, blk_out, half_out, n_out, blk_ref, half_ref, order_ref, chosen_ref, *flat
 ):
     _, blocks, width = pos_ref.shape
@@ -430,7 +435,16 @@
         return carry
 
     lax.fori_loop(0, blocks + PAD, home_item, 0)
-    run_items((blocks + KI - 1) // KI, blk_ref, half_ref, nact_ref, fc_ref, tab_ref, acc_ref, take_buffers(flat))
+    run_items(
+        (blocks + KI - 1) // KI,
+        blk_ref,
+        half_ref,
+        nact_ref,
+        fc_ref,
+        lambda one: mine_ref[one] + theirs_ref[one],
+        acc_ref,
+        take_buffers(flat),
+    )
 
     most = slot_ref.shape[1] // blocks
     lists = 128 // 2
@@ -484,7 +498,7 @@
         half_ref,
         nact_ref,
         fc_ref,
-        tab_ref,
+        lambda one: tab_ref[one],
         acc_ref,
         take_buffers(flat),
         copy.wait,
@@ -546,14 +560,12 @@
 
     mine = build_lists(held, node_lists, list_counts)
     theirs = lax.ppermute(mine, "sub", [(i, i ^ 1) for i in range(sharers)])
-    tab, reply = pl.pallas_call(
+    reply = pl.pallas_call(
         pack_kernel,
-        out_shape=(
-            jax.ShapeDtypeStruct((lists, 8, 128), F32),
-            jax.ShapeDtypeStruct((domains, SLOTS, 8, 128), F32),
-        ),
+        out_shape=jax.ShapeDtypeStruct((domains, SLOTS, 8, 128), F32),
         in_specs=[sspec(), vspec(), vspec()],
-        out_specs=(vspec(),) * 2,
+        out_specs=hspec(),
+        scratch_shapes=[VMEM((domains, SLOTS, 8, 128), F32), pltpu.SemaphoreType.DMA((4,))],
         compiler_params=pltpu.CompilerParams(vmem_limit_bytes=60 << 20),
         name="pack",
     )(req, mine, theirs)
@@ -571,13 +583,13 @@
             jax.ShapeDtypeStruct((2 * room,), I32),
             jax.ShapeDtypeStruct((8,), I32),
         ),
-        in_specs=[sspec()] * 5 + [vspec()] * 3,
+        in_specs=[sspec()] * 5 + [vspec()] * 4,
         out_specs=(vspec(),) * 3 + (sspec(),) * 3,
         scratch_shapes=[SMEM((blocks + PAD,), I32), SMEM((2 * (blocks + PAD),), I32), SMEM((blocks + 1,), I32), VMEM((4, width, width), BF16), *buffers()],
         compiler_params=pltpu.CompilerParams(vmem_limit_bytes=65136 << 10),
         cost_estimate=pl.CostEstimate(flops=40_000_000, bytes_accessed=4_000_000, transcendentals=12_000_000),
         name="home_pulls",
-    )(home_groups, slot, target_groups.T, req, nact, positions, time_bins, tab)
+    )(home_groups, slot, target_groups.T, req, nact, positions, time_bins, mine, theirs)
 
     out = pl.pallas_call(
         remote_kernel,

time: 106 us -> 105 us (level)
  Pallas kernels: 65.1 us -> 62.7 us
    pallas_call x1, Pallas kernels: 23.6 us -> 22.3 us  [forces_of(): pl.pallas_call(home_kernel, out_shape=(jax.ShapeDtypeStruct((blocks, 32,...]
  transfers between devices with their start and end apart: 5 -> 5, of which waited for: 4 -> 4; matrix products, arithmetic and copies ran while one was open for 0% -> 0% of each run, Pallas kernels for 22% -> 21%
where the time goes in v3:
time: 105 us; the launch traced here: 104 us
  Pallas kernels  62.7 us (60%)
  blocking collectives  21.4 us (20%)
  waiting for transfers between devices  10.7 us (10%)
  starting transfers between devices  7.77 us (7%)
  local copies, waits for them, and re-layouts  1.33 us (1%)
    pallas_call x1, Pallas kernels, forces_of(): pl.pallas_call(remote_kernel, out_shape=jax.ShapeDtypeStruct((3, blocks,...  27 us
    pallas_call x1, Pallas kernels, forces_of(): pl.pallas_call(home_kernel, out_shape=(jax.ShapeDtypeStruct((blocks, 32,...  22.3 us
    all_to_all x1, blocking collectives, forces_of(): req = lax.all_to_all(req.reshape(domains, 1, 128), 'dom', 0, 0, tiled=True)  21.4 us
    pallas_call x1, Pallas kernels, build_lists(): pl.pallas_call(list_kernel, out_shape=jax.ShapeDtypeStruct((lists, 8, 128...  9.25 us
    all_to_all x1, waiting for transfers between devices, forces_of(): lax.all_to_all(reply.reshape(domains, SLOTS * 8, 128), 'dom', 0, 0, tiled...  5.69 us
    ppermute x3, waiting for transfers between devices, forces_of(): lax.ppermute(nodes, 'sub', [(i, (i + 2 * j) % sharers) for i in range(sha...  4.99 us
    all_to_all x1, starting transfers between devices, forces_of(): lax.all_to_all(reply.reshape(domains, SLOTS * 8, 128), 'dom', 0, 0, tiled...  4.86 us
    ppermute x3, starting transfers between devices, forces_of(): lax.ppermute(nodes, 'sub', [(i, (i + 2 * j) % sharers) for i in range(sha...  2.81 us
  transfers between devices with their start and end apart: 5, of which 4 were waited for; matrix products, arithmetic and copies ran while one was open for 0% of the time, Pallas kernels for 21%

profile of v3, /device:TPU:0, one launch (start us, length us, event | category | flops | bytes accessed | tf_op | source)
XLA Modules:
  0.0 104.1 jit_solution(8511975578500287665)
XLA Ops:
  0.0 1.9 %requests.1 = (s32[32,128]{1,0:T(8,128)}, s32[1,256]{1,0:T(1,128)}, s32[1,64]{1,0:T(1,128)}, f32[4,32,128]{2,1,0:T(8,128)}) custom-call(s32[4,64]{1,0:T(4,128)} %bitcast.20, s32[4,64]{1,0:T(4,128)} %bitcast.21, s32[1,64]{1,0:T(1,128)} %bitcast.23, f32[3,4096]{1,0:T(4,128)} %refs_3_.1, f32[1,4096]{1,0:T(1,128)} %bitcast.18, s32[64,256]{1,0:T(8,128)} %bins_ref.1), custom_call_target="tpu_custom_call" | custom-call | tf_op jit(solution)/shard_map/requests/pallas_call | solution.py:540
  1.9 1.1 %collective-permute-start.2 = (f32[4,32,128]{2,1,0:T(8,128)}, f32[4,32,128]{2,1,0:T(8,128)S(1)}, u32[]{:S(2)}, u32[]{:S(2)}) collective-permute-start(f32[4,32,128]{2,1,0:T(8,128)} %get-tuple-element.18.refs_0_), channel_id=1, source_target_pairs={{0,6},{1,7},{2,0},{3,1},{4,2},{5,3},{6,4},{7,5},{8,14},{9,15},{10,... | collective-permute-start | bytes 196616 | tf_op jit(solution)/shard_map/ppermute | solution.py:556
  3.1 0.8 collective-permute-start.1
  3.9 0.9 collective-permute-start
  4.8 1.7 %collective-permute-done.2.refs_3_ = f32[4,32,128]{2,1,0:T(8,128)S(1)} collective-permute-done((f32[4,32,128]{2,1,0:T(8,128)}, f32[4,32,128]{2,1,0:T(8,128)S(1)}, u32[]{:S(2)}, u32[]{:S(2)}) %collective-permute-start.2) | collective-permute-done | bytes 65568 | tf_op jit(solution)/shard_map/ppermute | solution.py:556
  6.5 0.0 copy-start.1
  6.5 2.6 %collective-permute-done.1.refs_2_ = f32[4,32,128]{2,1,0:T(8,128)S(1)} collective-permute-done((f32[4,32,128]{2,1,0:T(8,128)}, f32[4,32,128]{2,1,0:T(8,128)S(1)}, u32[]{:S(2)}, u32[]{:S(2)}) %collective-permute-start.1) | collective-permute-done | bytes 65568 | tf_op jit(solution)/shard_map/ppermute | solution.py:556
  9.1 0.0 copy-start.2
  9.1 0.7 collective-permute-done.refs_1_
  9.8 0.0 copy-done.1
  9.8 0.0 copy-done.2
  9.8 0.0 copy-start.3
  9.8 0.6 copy-done.3
  10.4 9.2 %lists.1.mine_ref = f32[64,8,128]{2,1,0:T(8,128)} custom-call(f32[4,32,128]{2,1,0:T(8,128)} %get-tuple-element.18.refs_0_, f32[4,32,128]{2,1,0:T(8,128)} %copy-done.3, f32[4,32,128]{2,1,0:T(8,128)} %copy-done.2, f32[4,32,128]{2,1,0:T(8,128)} %copy-done.1, s32[64,256]{1,0:T(8,128)} %refs_4_.1, s32[64]{0:T(128)} %refs_5_.3), custom_call_target="tpu_custom_call" | custom-call | flops 20000000 | bytes 1000000 | tf_op jit(solution)/shard_map/lists/pallas_call | solution.py:166
  19.6 0.1 collective-permute-start.3
  19.7 21.4 %all_to_all.10 = s32[32,1,128]{2,1,0:T(1,128)} all-to-all(s32[32,1,128]{2,1,0:T(1,128)} %bitcast.19), channel_id=1, replica_groups=mesh['dom'=32,'sub'=8] {'dom'}, dimensions={0} | all-to-all | bytes 32768 | tf_op jit(solution)/shard_map/all_to_all | solution.py:557
  41.1 0.0 collective-permute-done.3.theirs_ref
  41.1 0.0 copy-start
  41.1 0.7 copy-done
  41.9 2.2 %pack.1 = f32[32,8,8,128]{3,2,1,0:T(8,128)} custom-call(s32[32,128]{1,0:T(8,128)} %bitcast.16, f32[64,8,128]{2,1,0:T(8,128)} %lists.1.mine_ref, f32[64,8,128]{2,1,0:T(8,128)} %copy-done), custom_call_target="tpu_custom_call" | custom-call | tf_op jit(solution)/shard_map/pack/pallas_call | solution.py:563
  44.1 4.9 %all-to-all-start.1 = ((f32[32,64,128]{2,1,0:T(8,128)}), f32[32,64,128]{2,1,0:T(8,128)}, u32[]{:S(2)}, u32[]{:S(2)}) async-start(f32[32,64,128]{2,1,0:T(8,128)} %bitcast.13), calls=%async_computation.1 | async-start | bytes 2097152 | tf_op jit(solution)/shard_map/all_to_all | solution.py:572
  49.0 22.3 %home_pulls.1 = (bf16[64,32,256]{2,1,0:T(8,128)(2,1)}, s32[64,256]{1,0:T(8,128)}, f32[65,16,256]{2,1,0:T(8,128)}, s32[288]{0:T(512)}, s32[576]{0:T(1024)}, /*index=5*/s32[8]{0:T(128)}) custom-call(s32[64]{0:T(128)} %home_ref.1, s32[1,256]{1,0:T(1,128)} %get-tuple-element.15.slot_ref, s32[4,64]{1,0:T(4,128)} %bitcast.22, s32[32,128]{1,0:T(8,128)} %bitcast.17, ...), custom_call_target="tpu_custom_call" | custom-call | flops 40000000 | bytes 4000000 | tf_op jit(solution)/shard_map/home_pulls/pallas_call | solution.py:576
  71.2 5.7 %all-to-all-done.1 = f32[32,64,128]{2,1,0:T(8,128)} async-done(((f32[32,64,128]{2,1,0:T(8,128)}), f32[32,64,128]{2,1,0:T(8,128)}, u32[]{:S(2)}, u32[]{:S(2)}) %all-to-all-start.1) | async-done | bytes 1048608 | tf_op jit(solution)/shard_map/all_to_all | solution.py:572
  76.9 27.0 %remote_pulls.1 = f32[3,64,256]{2,1,0:T(8,128)} custom-call(s32[8]{0:T(128)} %get-tuple-element.19.n_ref, s32[288]{0:T(512)} %get-tuple-element.20.blk_ref, s32[576]{0:T(1024)} %get-tuple-element.21.half_ref, s32[64]{0:T(128)} %bitcast.25, bf16[64,32,256]{2,1,0:T(8,128)(2,1)} %get-tuple-element.22.fc_ref, f32[256,8,128]{2,1,0:T(8,128)} %bitcast.10.tab_ref, ...), custom_call_target="tpu_custom_call" | custom-call | tf_op jit(solution)/shard_map/remote_pulls/pallas_call | solution.py:594
Async XLA Ops:
  1.9 4.6 %collective-permute-start.2 = (f32[4,32,128]{2,1,0:T(8,128)}, f32[4,32,128]{2,1,0:T(8,128)S(1)}, u32[]{:S(2)}, u32[]{:S(2)}) collective-permute-start(f32[4,32,128]{2,1,0:T(8,128)} %get-tuple-element.18.refs_0_), channel_id=1, source_target_pairs={{0,6},{1,7},{2,0},{3,1},{4,2},{5,3},{6,4},{7,5},{8,14},{9,15},{10,... | collective-permute-start | bytes 196616 | tf_op jit(solution)/shard_map/ppermute | solution.py:556
  3.1 6.0 %collective-permute-start.1 = (f32[4,32,128]{2,1,0:T(8,128)}, f32[4,32,128]{2,1,0:T(8,128)S(1)}, u32[]{:S(2)}, u32[]{:S(2)}) collective-permute-start(f32[4,32,128]{2,1,0:T(8,128)} %get-tuple-element.18.refs_0_), channel_id=1, source_target_pairs={{0,4},{1,5},{2,6},{3,7},{4,0},{5,1},{6,2},{7,3},{8,12},{9,13},{10,... | collective-permute-start | bytes 196616 | tf_op jit(solution)/shard_map/ppermute | solution.py:556
  3.9 5.9 %collective-permute-start = (f32[4,32,128]{2,1,0:T(8,128)}, f32[4,32,128]{2,1,0:T(8,128)S(1)}, u32[]{:S(2)}, u32[]{:S(2)}) collective-permute-start(f32[4,32,128]{2,1,0:T(8,128)} %get-tuple-element.18.refs_0_), channel_id=1, source_target_pairs={{0,2},{1,3},{2,4},{3,5},{4,6},{5,7},{6,0},{7,1},{8,10},{9,11},{10,... | collective-permute-start | bytes 196616 | tf_op jit(solution)/shard_map/ppermute | solution.py:556
  6.5 3.3 %copy-start.1 = (f32[4,32,128]{2,1,0:T(8,128)}, f32[4,32,128]{2,1,0:T(8,128)S(1)}, u32[]{:S(2)}) copy-start(f32[4,32,128]{2,1,0:T(8,128)S(1)} %collective-permute-done.2.refs_3_) | copy-start | bytes 196612
  9.1 0.7 copy-start.2
  9.8 0.6 copy-start.3
  19.6 21.5 %collective-permute-start.3 = (f32[64,8,128]{2,1,0:T(8,128)}, f32[64,8,128]{2,1,0:T(8,128)S(1)}, u32[]{:S(2)}, u32[]{:S(2)}) collective-permute-start(f32[64,8,128]{2,1,0:T(8,128)} %lists.1.mine_ref), channel_id=1, source_target_pairs={{0,1},{1,0},{2,3},{3,2},{4,5},{5,4},{6,7},{7,6},{8,9},{9,8},{10,11... | collective-permute-start | bytes 786440 | tf_op jit(solution)/shard_map/ppermute | solution.py:562
  41.1 0.7 copy-start
  44.1 32.8 %all-to-all-start.1 = ((f32[32,64,128]{2,1,0:T(8,128)}), f32[32,64,128]{2,1,0:T(8,128)}, u32[]{:S(2)}, u32[]{:S(2)}) async-start(f32[32,64,128]{2,1,0:T(8,128)} %bitcast.13), calls=%async_computation.1 | async-start | bytes 2097152 | tf_op jit(solution)/shard_map/all_to_all | solution.py:572
